TPU v7x, 128 devices: a whole 4x4x4 slice. The times are simulated.
128 devices in a mesh: vocab: 8 (over z, core), dp: 16 (over x, y).
Axes of the slice: x: 4, y: 4, z: 4, core: 2. Of those that a mesh axis runs over, the one named last changes fastest.
Arguments:
- hidden: bfloat16 [5632, 4096], P('dp'), may hold values from -240 to 240
- output_projection_weight: bfloat16 [4096, 32768], P('dp', 'vocab'), may hold values from -0.25 to 0.25
- adapter_down_weight: bfloat16 [4096, 128], replicated, may hold values from -0.09375 to 0.09375
- adapter_up_weight: bfloat16 [128, 32768], P(None, 'vocab'), may hold values from -0.75 to 0.75
- labels: int32 [5632], P('dp'), may hold values from 0 to 32767
- token_job_index: int32 [5632], P('dp'), may hold values from 0 to 7, as said below
Outputs:
- logits: bfloat16 [5632, 32768], P('dp', 'vocab')
- logit_gradient_rows: bfloat16 [5632, 32768], P('dp', 'vocab')
- hidden_state_gradient: bfloat16 [5632, 4096], P('dp')
- token_loss: float32 [5632], P('dp')
- job_loss: float32 [8], replicated
Inputs may be any that keep to these rules, and one draw needn't show every extreme that they name: `token_job_index`: a job may have no tokens at all, and the jobs' token counts differ widely.
All inputs are finite; a program needn't handle non-finite values.
Results may differ from a plain program's by a relative error of at most 0.014.
Values may be sent and summed in bfloat16 or wider, within the bound.
A program may use at most 256 MiB of HBM per device.

v0:
```python
import jax
import jax.numpy as jnp
from jax import lax
from jax.sharding import Mesh
from jax.sharding import PartitionSpec as P

ADAPTER_JOBS = 8
ADAPTER_RANK = 16
DP = ("dp_0", "dp_1")


def one_axis_at_a_time(shard, axes):
    for axis in axes:
        shard = lax.psum(shard, axis)
    return shard


def from_everyone(shard, axis):
    count = lax.axis_size(axis)
    return lax.all_to_all(
        jnp.broadcast_to(shard[None], (count, *shard.shape)), axis, 0, 0, tiled=True
    )


def all_in_one(shard, axis):
    leaves = jax.tree.leaves(shard)
    turns = sorted(range(len(leaves)), key=lambda k: -leaves[k].size)
    width = (1, *leaves[turns[0]].shape)[-1]
    lines = [
        jnp.pad(leaves[k].reshape(-1), (0, -leaves[k].size % width)).reshape(-1, width)
        for k in turns
    ]
    both, at, found = (from_everyone(jnp.concatenate(lines), axis), 0, {})
    for k, line in zip(turns, lines):
        section = both[:, at : at + len(line)].reshape(len(both), -1)
        found[k] = section[:, : leaves[k].size].reshape(-1, *leaves[k].shape)
        at += len(line)
    numbers = iter(range(len(leaves)))
    return jax.tree.map(lambda _: found[next(numbers)], shard)


def folded_in_pairs(pieces, combine):
    while len(jax.tree.leaves(pieces)[0]) > 1:
        pieces = jax.vmap(combine)(
            *(jax.tree.map(lambda part: part[side::2], pieces) for side in (0, 1))
        )
    return jax.tree.map(lambda part: part[0], pieces)


def combined_all(shard, axis, combine):
    pieces = all_in_one(shard, axis)
    return folded_in_pairs(pieces, combine)


def combine_stats(left_side, right_side):
    left_max, left_sum, left_target = left_side
    right_max, right_sum, right_target = right_side
    joint_max = jnp.maximum(left_max, right_max)
    joint_sum = left_sum * jnp.exp(left_max - joint_max) + right_sum * jnp.exp(
        right_max - joint_max
    )
    return (joint_max, joint_sum, left_target + right_target)


def shards(
    hidden,
    output_projection_weight,
    adapter_down_weight,
    adapter_up_weight,
    labels,
    token_job_index,
):
    row_count = hidden.shape[0]
    vocabulary_columns = adapter_up_weight.shape[1]
    adapter_job_columns = adapter_down_weight.shape[1]
    col_start = lax.axis_index("vocab") * vocabulary_columns
    col_job = lax.iota(jnp.int32, adapter_job_columns) // ADAPTER_RANK
    adapter_job_mask = (token_job_index[:, None] == col_job[None, :]).astype(jnp.float32)
    adapter_input = (
        jnp.dot(hidden, adapter_down_weight, preferred_element_type=jnp.float32) * adapter_job_mask
    ).astype(jnp.bfloat16)
    adapter_logit_portion = jnp.dot(
        adapter_input, adapter_up_weight, preferred_element_type=jnp.float32
    )
    full_weight = lax.all_gather(output_projection_weight, DP, axis=0, tiled=True)
    frozen_logit_rows = jnp.dot(hidden, full_weight, preferred_element_type=jnp.float32)
    complete_logit_rows = frozen_logit_rows + adapter_logit_portion
    onehot = (token_job_index[:, None] == lax.iota(jnp.int32, ADAPTER_JOBS)[None, :]).astype(
        jnp.float32
    )
    counts = one_axis_at_a_time(jnp.sum(onehot, axis=0), DP)
    per_job = row_count * lax.axis_size(DP) / (ADAPTER_JOBS * jnp.maximum(counts, 1.0))
    token_weight = jnp.sum(onehot * per_job[None, :], axis=1)
    local_label = labels - col_start
    target_hit = lax.iota(jnp.int32, vocabulary_columns)[None, :] == local_label[:, None]
    target_part = jnp.sum(jnp.where(target_hit, complete_logit_rows, 0.0), axis=1)
    local_max = jnp.max(complete_logit_rows, axis=1)
    local_sum = jnp.sum(jnp.exp(complete_logit_rows - local_max[:, None]), axis=1)
    row_max, exp_total, target = combined_all(
        (local_max, local_sum, target_part), "vocab", combine_stats
    )
    shifted = jnp.exp(complete_logit_rows - row_max[:, None])
    token_loss = row_max + jnp.log(exp_total) - target
    logit_gradient_rows = (
        token_weight[:, None] * (shifted / exp_total[:, None] - target_hit.astype(jnp.float32))
    ).astype(jnp.bfloat16)
    job_sums = one_axis_at_a_time(jnp.sum(onehot * token_loss[:, None], axis=0), DP)
    job_loss = job_sums / jnp.maximum(counts, 1.0)
    adapter_gradient = jnp.einsum(
        "ba,fa->bf", logit_gradient_rows, adapter_up_weight, preferred_element_type=jnp.float32
    )
    grad_terms = jnp.einsum(
        "tv,dv->td", logit_gradient_rows, full_weight, preferred_element_type=jnp.float32
    )
    grad_terms = grad_terms + jnp.dot(
        adapter_gradient * adapter_job_mask,
        adapter_down_weight.astype(jnp.float32).T,
        precision=lax.Precision.HIGHEST,
    )
    share = lax.psum_scatter(
        grad_terms.astype(jnp.bfloat16), "vocab", scatter_dimension=1, tiled=True
    )
    hidden_state_gradient = lax.all_gather(share, "vocab", axis=1, tiled=True)
    return (
        complete_logit_rows.astype(jnp.bfloat16),
        logit_gradient_rows,
        hidden_state_gradient,
        token_loss,
        job_loss,
    )


def solution(mesh):
    split = Mesh(mesh.devices.reshape(mesh.shape["vocab"], 4, 4), ("vocab", "dp_0", "dp_1"))
    return jax.shard_map(
        shards,
        mesh=split,
        in_specs=(P(DP, None), P(DP, "vocab"), P(), P(None, "vocab"), P(DP), P(DP)),
        out_specs=(P(DP, "vocab"), P(DP, "vocab"), P(DP, None), P(DP), P()),
        check_vma=False,
    )
```

profile of v0, /device:TPU:1, one launch (start us, length us, event | category | flops | bytes accessed | tf_op | source)
XLA Modules:
  0.0 360.4 jit_solution(2761675084552903200)
XLA Ops:
  7.2 0.7 all-gather.3.cloned.1.call-update
  7.9 0.9 convert_reduce_fusion
  8.8 9.3 %psum.28 = f32[8]{0:T(128)S(1)} all-reduce(f32[8]{0:T(128)S(1)} %convert_reduce_fusion), channel_id=1, replica_groups=mesh['vocab'=8,'dp_0'=4,'dp_1'=4] {'dp_0'}, use_global_device_ids=true, to_apply=%region_1.2 | all-reduce | flops 8 | bytes 64 | tf_op jit(solution)/shard_map/psum | solution.py:14
  18.1 9.0 %psum.29 = f32[8]{0:T(128)S(1)} all-reduce(f32[8]{0:T(128)S(1)} %psum.28), channel_id=1, replica_groups=mesh['vocab'=8,'dp_0'=4,'dp_1'=4] {'dp_1'}, use_global_device_ids=true, to_apply=%region_2.3 | all-reduce | flops 8 | bytes 64 | tf_op jit(solution)/shard_map/psum | solution.py:14
  27.1 0.7 broadcast_subtract_fusion
  27.8 182.3 %all-gather.3.cloned.1.call-done = bf16[4096,4096]{1,0:T(8,128)(2,1)} async-done(((bf16[256,4096]{1,0:T(8,128)(2,1)}), bf16[4096,4096]{1,0:T(8,128)(2,1)}) %all-gather.3.cloned.1.call-update) | async-done | bytes 33554448 | tf_op jit(solution)/shard_map/all_gather | solution.py:85
  210.0 18.8 %fusion.12 = f32[352,4096]{1,0:T(8,128)} fusion(bf16[352,4096]{1,0:T(8,128)(2,1)S(1)} %copy-done, bf16[4096,4096]{1,0:T(8,128)(2,1)} %all-gather.3.cloned.1.call-done), kind=kOutput, calls=%fused_computation.42 | convolution fusion | flops 11811160064 | bytes 42205184 | tf_op jit(solution)/shard_map/dot_general | solution.py:86
  228.8 9.0 %fusion.11 = (f32[352]{0:T(512)S(1)}, f32[352,4096]{1,0:T(8,128)}) fusion(f32[352,4096]{1,0:T(8,128)} %fusion.12, bf16[128,4096]{1,0:T(8,128)(2,1)} %param.9, bf16[352,4096]{1,0:T(8,128)(2,1)S(1)} %copy-done, bf16[4096,128]{1,0:T(8,128)(2,1)} %param.8, s32[128]{0:T(128)S(1)} %and_select_fusion, s32[352]{0:T(512)S(1)} %copy-done.4), kind=kOutput, calls=%fused_computation.41 | convolution fusion | flops 741215872 | bytes 16518400 | tf_op jit(solution)/shard_map/dot_general | solution.py:82
  237.8 4.2 %exponential_reduce_fusion = (f32[352]{0:T(512)S(1)}, f32[352]{0:T(512)S(1)}) fusion(f32[352,4096]{1,0:T(8,128)} %get-tuple-element.21, f32[352]{0:T(512)S(1)} %get-tuple-element.20, s32[352]{0:T(512)S(1)} %broadcast_subtract_fusion), kind=kLoop, calls=%fused_computation.5 | loop fusion | flops 7208256 | bytes 5772800 | tf_op jit(solution)/shard_map/reduce_sum | solution.py:98
  242.1 0.6 broadcast_in_dim.6
  242.7 5.3 %all-to-all-start = ((f32[8,3,352]{2,1,0:T(4,128)}), f32[8,3,352]{2,1,0:T(4,128)S(1)}, u32[]{:S(2)}, u32[]{:S(2)}) async-start(f32[8,3,352]{2,1,0:T(4,128)} %broadcast_in_dim.6), calls=%async_computation | async-start | bytes 98304 | tf_op jit(solution)/shard_map/all_to_all | solution.py:20
  248.0 4.8 %all-to-all-done = f32[8,3,352]{2,1,0:T(4,128)S(1)} async-done(((f32[8,3,352]{2,1,0:T(4,128)}), f32[8,3,352]{2,1,0:T(4,128)S(1)}, u32[]{:S(2)}, u32[]{:S(2)}) %all-to-all-start) | async-done | bytes 33824 | tf_op jit(solution)/shard_map/all_to_all | solution.py:20
  253.2 0.1 select_reduce_fusion.1
  253.4 7.8 %multiply_convert_fusion = (bf16[352,4096]{1,0:T(8,128)(2,1)S(1)}, bf16[352,4096]{1,0:T(8,128)(2,1)}) fusion(f32[352,4096]{1,0:T(8,128)} %get-tuple-element.21, f32[352]{0:T(512)S(1)} %get-tuple-element.8, f32[352]{0:T(512)S(1)} %get-tuple-element.7, s32[352]{0:T(512)S(1)} %broadcast_subtract_fusion, f32[352]{0:T(512)S(1)} %get-tuple-element.10), kind=kLoop, calls=%fused_computation.2 | loop fusion | flops 11534336 | bytes 11539968 | tf_op jit(solution)/shard_map/convert_element_type | solution.py:106
  261.2 0.9 convolution_select_fusion
  262.1 0.7 copy-done.2
  262.8 18.9 %fusion.13 = f32[352,4096]{1,0:T(8,128)} fusion(bf16[352,4096]{1,0:T(8,128)(2,1)S(1)} %get-tuple-element.30, bf16[4096,4096]{1,0:T(8,128)(2,1)} %all-gather.3.cloned.1.call-done), kind=kOutput, calls=%fused_computation.43 | convolution fusion | flops 11811160064 | bytes 42205184 | tf_op jit(solution)/shard_map/tv,dv->td/dot_general | solution.py:112
  281.6 7.2 %fusion = bf16[352,4096]{1,0:T(8,128)(2,1)} fusion(f32[352,4096]{1,0:T(8,128)} %fusion.13, f32[352,128]{1,0:T(8,128)S(1)} %convolution_select_fusion, bf16[4096,128]{1,0:T(8,128)(2,1)} %param.8), kind=kOutput, calls=%fused_computation.6 | convolution fusion | flops 2217476096 | bytes 9879552 | tf_op jit(solution)/shard_map/dot_general | solution.py:115
  288.9 30.4 %reduce-scatter.2.cloned.1.call-done = bf16[352,512]{1,0:T(8,128)(2,1)} async-done(((bf16[352,4096]{1,0:T(8,128)(2,1)}), bf16[352,512]{1,0:T(8,128)(2,1)}) %reduce-scatter.2.cloned.1.call-update) | async-done | bytes 360464 | tf_op jit(solution)/shard_map/reduce_scatter | solution.py:120
  319.3 8.5 %psum.30 = f32[8]{0:T(128)S(1)} all-reduce(f32[8]{0:T(128)S(1)} %get-tuple-element.9), channel_id=1, replica_groups=mesh['vocab'=8,'dp_0'=4,'dp_1'=4] {'dp_0'}, use_global_device_ids=true, to_apply=%region_9.10 | all-reduce | flops 8 | bytes 64 | tf_op jit(solution)/shard_map/psum | solution.py:14
  327.8 8.5 %psum.31 = f32[8]{0:T(128)S(1)} all-reduce(f32[8]{0:T(128)S(1)} %psum.30), channel_id=1, replica_groups=mesh['vocab'=8,'dp_0'=4,'dp_1'=4] {'dp_1'}, use_global_device_ids=true, to_apply=%region_10.11 | all-reduce | flops 8 | bytes 64 | tf_op jit(solution)/shard_map/psum | solution.py:14
  336.3 0.5 maximum_divide_fusion
  336.8 13.3 %all-gather.5.cloned.1.call-done = bf16[352,4096]{1,0:T(8,128)(2,1)} async-done(((bf16[352,512]{1,0:T(8,128)(2,1)}), bf16[352,4096]{1,0:T(8,128)(2,1)}) %all-gather.5.cloned.1.call-update) | async-done | bytes 2883600 | tf_op jit(solution)/shard_map/all_gather | solution.py:123
  350.1 3.7 %copy.21 = bf16[352,4096]{1,0:T(8,128)(2,1)} copy(bf16[352,4096]{1,0:T(8,128)(2,1)} %all-gather.5.cloned.1.call-done) | data formatting | bytes 5767168
  (44 shorter events, 0.6 us)
Async XLA Ops:
  7.2 202.9 %copy-start = (bf16[352,4096]{1,0:T(8,128)(2,1)S(1)}, bf16[352,4096]{1,0:T(8,128)(2,1)}, u32[]{:S(2)}) copy-start(bf16[352,4096]{1,0:T(8,128)(2,1)} %param.6) | copy-start | bytes 8650756
  7.2 202.9 %all-gather.3.cloned.1.call-start = ((), (), s32[]{:S(2)}) async-start(), calls=%async_computation.2 | async-start | bytes 35651584 | tf_op jit(solution)/shard_map/all_gather | solution.py:85
  27.8 201.1 %copy-start.4 = (s32[352]{0:T(512)S(1)}, s32[352]{0:T(512)}, u32[]{:S(2)}) copy-start(s32[352]{0:T(512)} %param.11) | copy-start | bytes 4228
  242.7 10.0 %all-to-all-start = ((f32[8,3,352]{2,1,0:T(4,128)}), f32[8,3,352]{2,1,0:T(4,128)S(1)}, u32[]{:S(2)}, u32[]{:S(2)}) async-start(f32[8,3,352]{2,1,0:T(4,128)} %broadcast_in_dim.6), calls=%async_computation | async-start | bytes 98304 | tf_op jit(solution)/shard_map/all_to_all | solution.py:20
  248.0 71.3 %reduce-scatter.2.cloned.1.call-start = ((), (), s32[]{:S(2)}) async-start(), calls=%async_computation.3 | async-start | bytes 3244032 | tf_op jit(solution)/shard_map/reduce_scatter | solution.py:120
  253.2 8.0 %copy-start.5 = (f32[352]{0:T(512)}, f32[352]{0:T(512)S(1)}, u32[]{:S(2)}) copy-start(f32[352]{0:T(512)S(1)} %add_subtract_fusion) | copy-start | bytes 4228
  253.4 7.8 %copy-start.3 = (bf16[128,4096]{1,0:T(8,128)(2,1)S(1)}, bf16[128,4096]{1,0:T(8,128)(2,1)}, u32[]{:S(2)}) copy-start(bf16[128,4096]{1,0:T(8,128)(2,1)} %param.9) | copy-start | bytes 3145732
  261.2 1.6 copy-start.2
  281.6 72.2 %copy-start.1 = (bf16[352,4096]{1,0:T(8,128)(2,1)S(1)}, bf16[352,4096]{1,0:T(8,128)(2,1)}, u32[]{:S(2)}) copy-start(bf16[352,4096]{1,0:T(8,128)(2,1)} %param.6) | copy-start | bytes 8650756
  288.9 61.2 %all-gather.5.cloned.1.call-start = ((), (), s32[]{:S(2)}) async-start(), calls=%async_computation.4 | async-start | bytes 3244032 | tf_op jit(solution)/shard_map/all_gather | solution.py:123
Sparse Core Ops, SparseCore 0:
  10.1 199.8 all-gather.2
  289.0 30.2 reduce-scatter.1
  321.0 29.0 all-gather.4
where the time goes:
time: 361 us; the launch traced here: 360 us
  waiting for transfers between devices  231 us (64%)
  matrix products  54.7 us (15%)
  blocking collectives  35.2 us (10%)
  other arithmetic  14.4 us (4%)
  between operations  13.8 us (4%)
  local copies, waits for them, and re-layouts  5.36 us (1%)
  starting transfers between devices  5.34 us (1%)
    all_gather x1, waiting for transfers between devices, shards(): lax.all_gather(output_projection_weight, DP, axis=0, tiled=True)  182 us
    psum x4, blocking collectives, one_axis_at_a_time(): shard = lax.psum(shard, axis)  35.2 us
    reduce_scatter x1, waiting for transfers between devices, shards(): lax.psum_scatter(grad_terms.astype(jnp.bfloat16), 'vocab', scatter_dimens...  30.4 us
    dot_general x1, matrix products, shards(): jnp.einsum('tv,dv->td', logit_gradient_rows, full_weight, preferred_eleme...  18.9 us
    dot_general x1, matrix products, shards(): jnp.dot(hidden, full_weight, preferred_element_type=jnp.float32)  18.8 us
    all_gather x1, waiting for transfers between devices, shards(): hidden_state_gradient = lax.all_gather(share, 'vocab', axis=1, tiled=True)  13.3 us
    dot_general x1, matrix products, shards(): jnp.dot(adapter_input, adapter_up_weight, preferred_element_type=jnp.floa...  8.95 us
    convert_element_type x1, other arithmetic, shards(): logit_gradient_rows = (token_weight[:, None] * (shifted / exp_total[:, No...  7.79 us
  transfers between devices with their start and end apart: 4, of which 4 were waited for; matrix products, arithmetic and copies ran while one was open for 1% of the time, Pallas kernels for 0%

commit v1 on v0

v1 whole, which is shorter than its diff:
```python
import functools

import jax
import jax.numpy as jnp
from jax import lax
from jax.experimental import pallas as pl
from jax.experimental.pallas import tpu as pltpu
from jax.sharding import Mesh
from jax.sharding import PartitionSpec as P

MESH = pl.DeviceIdType.MESH
F32 = jnp.float32
BF16 = jnp.bfloat16

JOBS = 8
RANK = 16
NX = NY = NZ = 4
NC = 2
T = 352
S = NX * T
HT = T // 2
D = 4096
DB = D // (NX * NY)
V = 4096
U = V // NX
CW = 256
NK = U // CW
SH = D // (NZ * NC)
TOKENS = S * NY
NB = S // 128


def fdot(a, b):
    return jnp.dot(a, b, preferred_element_type=F32)


def tdot(a, b):
    return lax.dot_general(a, b, (((1,), (1,)), ((), ())), preferred_element_type=F32)


def kernel(
    hid, w, ad, au, aux,
    lg, gr, hg, tl, jl,
    H, W5, WS, E, LT, G5, RC, RR, R0, XS, XR, FO, AG, COL, COL2, LI, AU, AX, STA, STB, JR, CN, JL,
    ssem, rsem, lsem,
):
    z, c, x, y = (lax.axis_index(a) for a in ("z", "c", "x", "y"))
    v = z * NC + c

    def al(i, m):
        return pl.multiple_of(i, m)

    def xn(r):
        return lax.rem(x + r, NX)

    def yn(r):
        return lax.rem(y + r, NY)

    def zn(r):
        return lax.rem(z + r, NZ)

    used = {"s": 0, "r": 0, "l": 0}

    def take(kind, n=1):
        at = used[kind]
        used[kind] = at + n
        return at

    pending = []

    def rcopy(src, dst, si, ri, dev):
        return pltpu.make_async_remote_copy(
            src_ref=src, dst_ref=dst, send_sem=ssem.at[si], recv_sem=rsem.at[ri],
            device_id=dev, device_id_type=MESH,
        )

    def send(src, dst, ri, dev, keep=pending):
        d = rcopy(src, dst, take("s"), ri, dev)
        d.start()
        keep.append(d)

    def got(dst, ri):
        rcopy(dst, dst, 0, ri, {"x": xn(1)}).wait_recv()

    def load(src, dst, keep):
        d = pltpu.make_async_copy(src, dst, lsem.at[take("l")])
        d.start()
        keep.append(d)

    def drain(keep):
        for d in keep:
            d.wait()
        keep.clear()

    def drain_sends(keep):
        for d in keep:
            d.wait_send()
        keep.clear()

    bar = pltpu.get_barrier_semaphore()
    peers = (
        [{"x": xn(r)} for r in (1, 2, 3)]
        + [{"y": yn(r)} for r in (1, 2, 3)]
        + [{"z": zn(a), "c": lax.rem(c + b, NC)} for a in range(NZ) for b in range(NC) if a or b]
    )
    for dev in peers:
        pl.semaphore_signal(bar, inc=1, device_id=dev, device_id_type=MESH)

    first, own_h, rest = [], [], []
    load(w, WS, first)
    for p in range(NX * NY):
        n = (p % NX) * NY + p // NX
        load(hid.at[:, pl.ds(n * DB, DB)], H.at[pl.ds(al(x * T, 16), T), pl.ds(p * DB, DB)], own_h)
    load(aux, AX.at[x], first)
    own_rows = pl.ds(al((y * NX + x) * DB, DB), DB)
    load(w.at[:, pl.ds(al(x * U, U), U)], W5.at[own_rows, pl.ds(0, U)], first)
    load(au.at[:, pl.ds(al(x * U, U), U)], AU, rest)
    for p in range(NX * NY):
        n = (p % NX) * NY + p // NX
        for q in range(2):
            load(
                ad.at[pl.ds(n * DB, DB), :],
                W5.at[pl.ds(p * DB, DB), pl.ds(U + q * 128, 128)],
                rest,
            )
    pl.semaphore_wait(bar, len(peers))

    ORDER = (1, 3, 2)
    wx = take("r", NK * 3)
    hx = take("r", 3)
    ax = take("r", 3)
    wy = take("r", NK * 4)
    hz = take("r", 3 * 4)
    hc = take("r", 3 * 5)

    def wblock(row, k):
        return W5.at[row, pl.ds(k * CW, CW)]

    def send_w(k):
        for r in ORDER:
            send(
                WS.at[:, pl.ds(al(xn(r) * U + k * CW, CW), CW)],
                wblock(own_rows, k), wx + k * 3 + r - 1, {"x": xn(r)},
            )

    drain(first)
    send_w(0)
    for r in ORDER:
        send(AX.at[x], AX.at[x], ax + r - 1, {"x": xn(r)})
    drain(own_h)
    hsends = []

    def hpiece(xb, share, lo=0, n=T):
        return H.at[pl.ds(al(xb * T + lo, 16), n), pl.ds(al(share * SH, SH), SH)]

    for r in ORDER:
        send(hpiece(x, v), hpiece(x, v), hx + r - 1, {"x": xn(r)}, hsends)
    for k in range(1, NK):
        send_w(k)

    def ysrc(dy, k, lo=0, n=NX * DB):
        return wblock(pl.ds(al(yn(dy) * (NX * DB) + lo, DB), n), k)

    HB = NX * DB // 2

    def w_own(k):
        for r in ORDER:
            row = pl.ds(al((y * NX + lax.rem(x + NX - r, NX)) * DB, DB), DB)
            got(wblock(row, k), wx + k * 3 + r - 1)
        send(ysrc(0, k), ysrc(0, k), wy + k * 4 + 0, {"y": yn(1)})
        send(ysrc(0, k), ysrc(0, k), wy + k * 4 + 1, {"y": yn(3)})

    def w_fwd(k):
        got(ysrc(3, k), wy + k * 4 + 0)
        send(ysrc(3, k, 0, HB), ysrc(3, k, 0, HB), wy + k * 4 + 2, {"y": yn(1)})
        got(ysrc(1, k), wy + k * 4 + 1)
        send(ysrc(1, k, HB, HB), ysrc(1, k, HB, HB), wy + k * 4 + 3, {"y": yn(3)})

    def w_end(k):
        got(ysrc(2, k, 0, HB), wy + k * 4 + 2)
        got(ysrc(2, k, HB, HB), wy + k * 4 + 3)

    other = {"c": 1 - c}

    def h_in(r):
        xb = lax.rem(x + NX - r, NX)
        got(hpiece(xb, v), hx + r - 1)
        mine = hpiece(xb, v)
        b = hz + (r - 1) * 4
        send(mine, mine, b + 0, {"z": zn(1)}, hsends)
        send(mine, mine, b + 1, {"z": zn(3)}, hsends)
        send(mine, mine, hc + (r - 1) * 5, other, hsends)

    def h_fwd(r):
        xb = lax.rem(x + NX - r, NX)
        b, d = hz + (r - 1) * 4, hc + (r - 1) * 5
        left, right = zn(3) * NC + c, zn(1) * NC + c
        got(hpiece(xb, left), b + 0)
        send(hpiece(xb, left, 0, HT), hpiece(xb, left, 0, HT), b + 2, {"z": zn(1)}, hsends)
        send(hpiece(xb, left), hpiece(xb, left), d + 1, other, hsends)
        got(hpiece(xb, right), b + 1)
        send(hpiece(xb, right, HT, HT), hpiece(xb, right, HT, HT), b + 3, {"z": zn(3)}, hsends)
        send(hpiece(xb, right), hpiece(xb, right), d + 2, other, hsends)

    def h_last(r):
        xb = lax.rem(x + NX - r, NX)
        b, d = hz + (r - 1) * 4, hc + (r - 1) * 5
        far = zn(2) * NC + c
        got(hpiece(xb, far, 0, HT), b + 2)
        send(hpiece(xb, far, 0, HT), hpiece(xb, far, 0, HT), d + 3, other, hsends)
        got(hpiece(xb, far, HT, HT), b + 3)
        send(hpiece(xb, far, HT, HT), hpiece(xb, far, HT, HT), d + 4, other, hsends)

    def h_end(r):
        xb = lax.rem(x + NX - r, NX)
        d = hc + (r - 1) * 5
        k = 1 - c
        got(hpiece(xb, v - c + k), d)
        got(hpiece(xb, zn(3) * NC + k), d + 1)
        got(hpiece(xb, zn(1) * NC + k), d + 2)
        got(hpiece(xb, zn(2) * NC + k, 0, HT), d + 3)
        got(hpiece(xb, zn(2) * NC + k, HT, HT), d + 4)

    w_own(0)
    for r in ORDER:
        h_in(r)
    w_own(1)
    w_fwd(0)
    h_fwd(1)
    w_own(2)
    h_fwd(3)
    h_last(1)
    w_fwd(1)
    h_fwd(2)
    h_last(3)
    w_own(3)

    for r in ORDER:
        got(AX.at[lax.rem(x + NX - r, NX)], ax + r - 1)
    sub = lax.broadcasted_iota(jnp.int32, (8, 128), 0).astype(F32)
    subi = lax.broadcasted_iota(jnp.int32, (8, 128), 0)
    counts = jnp.zeros((8, 128), F32)
    for xb in range(NX):
        for q in range(3):
            tile = AX[xb, q]
            n = min(128, T - q * 128)
            turned = jnp.concatenate([tile, jnp.zeros((120, 128), F32)], axis=0).T
            COL[pl.ds(xb * T + q * 128, n), :] = turned[:n]
            counts = counts + (tile[1:2, :] == sub).astype(F32)
    CN[y] = counts
    cn = take("r", 3)
    for r in (1, 3, 2):
        send(CN.at[y], CN.at[y], cn + r - 1, {"y": yn(r)})
    drain(rest)
    w_fwd(2)
    h_last(2)
    w_end(0)
    for r in ORDER:
        h_end(r)
    drain_sends(hsends)

    lane128 = lax.broadcasted_iota(jnp.int32, (T, 128), 1)
    rank_job = (lane128 // RANK).astype(F32)

    def lora_in(m, carry):
        rows = pl.ds(al(m * T, 16), T)
        hit = COL[rows, 1:2] == rank_job
        a = fdot(H[rows, :], W5[:, U : U + 128])
        LI[rows, :] = jnp.where(hit, a, 0.0).astype(BF16)
        return carry

    lax.fori_loop(0, NX, lora_in, 0)

    base = v * V + x * U
    lane_cw = lax.broadcasted_iota(jnp.int32, (T, CW), 1)
    lgs = take("r", NK * 3)
    outs = []
    my_cols = al(x * U, U)

    def forward(k):
        def step(m, carry):
            rows = pl.ds(al(m * T, 16), T)
            a = fdot(H[rows, :], W5[:, k * CW : (k + 1) * CW])
            a = a + fdot(LI[rows, :], AU[:, k * CW : (k + 1) * CW])
            LT[rows, k * CW : (k + 1) * CW] = a.astype(BF16)
            top = jnp.max(a, axis=1, keepdims=True)
            e = jnp.exp(a - top)
            E[k, rows, :] = e
            total = jnp.sum(e, axis=1, keepdims=True)
            cols = (lane_cw + (base + k * CW)).astype(F32)
            target = jnp.sum(jnp.where(cols == COL[rows, 0:1], a, 0.0), axis=1, keepdims=True)
            old = COL[rows, :]
            old = jnp.where(lane128 == 8 + k, top, old)
            old = jnp.where(lane128 == 12 + k, total, old)
            COL[rows, :] = jnp.where(lane128 == 16 + k, target, old)
            return carry

        lax.fori_loop(0, NX, step, 0)

    def send_logits(k):
        for r in ORDER:
            send(
                LT.at[pl.ds(al(xn(r) * T, 16), T), pl.ds(k * CW, CW)],
                lg.at[:, pl.ds(al(my_cols + k * CW, CW), CW)],
                lgs + k * 3 + r - 1, {"x": xn(r)},
            )
        load(
            LT.at[pl.ds(al(x * T, 16), T), pl.ds(k * CW, CW)],
            lg.at[:, pl.ds(al(my_cols + k * CW, CW), CW)], outs,
        )

    forward(0)
    send_logits(0)
    w_end(1)
    forward(1)
    send_logits(1)
    w_fwd(3)
    w_end(2)
    forward(2)
    send_logits(2)
    w_end(3)
    forward(3)

    def row_stats(b, carry):
        t = COL[pl.ds(al(b * 128, 128), 128), :].T
        m, s, g = t[8:12], t[12:16], t[16:20]
        top = jnp.max(m, axis=0, keepdims=True)
        s = jnp.sum(s * jnp.exp(m - top), axis=0, keepdims=True)
        g = jnp.sum(g, axis=0, keepdims=True)
        JR[b] = jnp.broadcast_to(t[1:2], (8, 128))
        STA[v, b] = jnp.where(subi == 0, top, jnp.where(subi == 1, s, jnp.where(subi == 2, g, 0.0)))
        return carry

    lax.fori_loop(0, NB, row_stats, 0)
    sa = take("r", 7)
    sb = take("r", 3)
    turns = [(a, b) for a in (2, 1, 3, 0) for b in range(NC) if a or b]
    for a, b in turns:
        dev = {"z": zn(a), "c": lax.rem(c + b, NC)}
        send(STA.at[v], STA.at[v], sa + a * NC + b - 1, dev)
    for a, b in turns:
        src = lax.rem(z + NZ - a, NZ) * NC + lax.rem(c + b, NC)
        got(STA.at[src], sa + a * NC + b - 1)

    def joined(parts):
        top = functools.reduce(jnp.maximum, [p[0:1] for p in parts])
        s = functools.reduce(jnp.add, [p[1:2] * jnp.exp(p[0:1] - top) for p in parts])
        g = functools.reduce(jnp.add, [p[2:3] for p in parts])
        return top, s, g

    def stage_b(b, carry):
        top, s, g = joined([STA[i, b] for i in range(NZ * NC)])
        STB[x, b] = jnp.where(subi == 0, top, jnp.where(subi == 1, s, jnp.where(subi == 2, g, 0.0)))
        return carry

    lax.fori_loop(0, NB, stage_b, 0)
    for r in (2, 1, 3):
        send(STB.at[x], STB.at[x], sb + r - 1, {"x": xn(r)})
    send_logits(3)
    for r in (1, 3, 2):
        got(CN.at[lax.rem(y + NY - r, NY)], cn + r - 1)
    counts = jnp.sum(CN[0] + CN[1] + CN[2] + CN[3], axis=1, keepdims=True)
    counts = jnp.maximum(counts, 1.0)
    per_job = TOKENS / (JOBS * counts)
    for r in (2, 1, 3):
        got(STB.at[lax.rem(x + NX - r, NX)], sb + r - 1)

    def finish(b, job_sums):
        top, s, g = joined([STB[i, b] for i in range(NX)])
        onehot = (JR[b] == sub).astype(F32)
        loss = top + jnp.log(s) - g
        weight = jnp.sum(onehot * per_job, axis=0, keepdims=True)
        tile = jnp.where(
            subi == 0, top,
            jnp.where(subi == 1, weight / s, jnp.where(subi == 2, weight, jnp.where(subi == 3, loss, 0.0))),
        )
        turned = jnp.concatenate([tile, jnp.zeros((120, 128), F32)], axis=0).T
        COL2[pl.ds(al(b * 128, 128), 128), :] = turned
        return job_sums + onehot * loss

    JL[y] = lax.fori_loop(0, NB, finish, jnp.zeros((8, 128), F32))
    jn = take("r", 3)
    for r in (1, 3, 2):
        send(JL.at[y], JL.at[y], jn + r - 1, {"y": yn(r)})
    tl[...] = COL2[pl.ds(al(x * T, 8), T), :]

    def gradient(m, carry):
        rows = pl.ds(al(m * T, 16), T)
        lab = COL[rows, 0:1]
        weight = COL2[rows, 2:3]
        for k in range(NK):
            f = jnp.exp(COL[rows, 8 + k : 9 + k] - COL2[rows, 0:1]) * COL2[rows, 1:2]
            cols = (lane_cw + (base + k * CW)).astype(F32)
            g = E[k, rows, :] * f - jnp.where(cols == lab, weight, 0.0)
            G5[m, :, k * CW : (k + 1) * CW] = g.astype(BF16)
        part = tdot(G5[m, :, 0:U], AU[...])
        part = jnp.where(COL[rows, 1:2] == rank_job, part, 0.0)
        high = part.astype(BF16)
        G5[m, :, U : U + 128] = high
        G5[m, :, U + 128 : U + 256] = (part - high.astype(F32)).astype(BF16)
        return carry

    lax.fori_loop(0, NX, gradient, 0)
    grs = take("r", 3)
    for r in ORDER:
        send(G5.at[xn(r), :, pl.ds(0, U)], gr.at[:, pl.ds(my_cols, U)], grs + r - 1, {"x": xn(r)})
    load(G5.at[x, :, pl.ds(0, U)], gr.at[:, pl.ds(my_cols, U)], outs)

    cs_s, cs_r = take("s", 16), take("r", 16)
    ring_s, ring_r = take("s", 12), take("r", 12)

    def zt(s, h):
        return lax.rem(z + NZ + (2 * h - 1) * (s + 1), NZ)

    def unit(s, h, j, core):
        at = al((zt(s, h) * NC + core) * SH + h * CW, CW)
        g = G5[:, pl.ds(al(j * HT, 16), HT), :].reshape(NX * HT, U + 256)
        return tdot(g, W5[pl.ds(at, CW), :])

    def ps(i):
        return H.at[pl.ds(al(lax.rem(i, 2) * (S // 2), 16), S // 2), pl.ds(al(i // 2 * CW, CW), CW)]

    def ps_copy(i):
        return rcopy(ps(i), RC.at[i], cs_s + i, cs_r + i, other)

    def for_core(s):
        def step(q, carry):
            j, h = q // 2, lax.rem(q, 2)
            i = s * 4 + h * 2 + j
            ps(i)[...] = unit(s, h, j, 1 - c).astype(BF16)
            ps_copy(i).start()
            return carry

        lax.fori_loop(0, 4, step, 0)

    def ring_copy(s, h, j):
        i = h * 2 + j
        src = R0.at[i] if s == 0 else RR.at[(s - 1) * 4 + i]
        return rcopy(
            src, RR.at[s * 4 + i], ring_s + s * 4 + i, ring_r + s * 4 + i,
            {"z": lax.rem(z + NZ + 1 - 2 * h, NZ)},
        )

    def own_step(s, h, j):
        i = h * 2 + j
        a = unit(s, h, j, c)
        ps_copy(s * 4 + i).wait_recv()
        a = a + RC[s * 4 + i].astype(F32)
        if s:
            ring_copy(s - 1, h, j).wait_recv()
            a = a + RR[(s - 1) * 4 + i].astype(F32)
        return a

    def own(s):
        def step(q, carry):
            j, h = q // 2, lax.rem(q, 2)
            i = h * 2 + j
            a = own_step(s, h, j).astype(BF16)
            if s == 0:
                R0[i] = a
            else:
                RR[(s - 1) * 4 + i] = a
            ring_copy(s, h, j).start()
            return carry

        lax.fori_loop(0, 4, step, 0)

    for_core(0)
    for_core(1)
    own(0)
    for_core(2)
    own(1)
    for_core(3)
    own(2)

    xr = take("r", 6)
    ag = take("r", 6)
    cc = take("r", 4 + 12)

    def hg_cols(zz, core, h):
        return pl.ds(al(((NC * core + h) * NY + zz) * DB, DB), DB)

    def spread(src, zz, j, sem):
        for h in range(2):
            piece = src.at[:, pl.ds(h * CW, CW)]
            dst = hg.at[pl.ds(j * HT, HT), hg_cols(zz, c, h)]
            send(piece, dst, sem + h, other)
            load(piece, dst, outs)

    for j in range(2):
        for h in range(2):
            XS[j, :, :, h * CW : (h + 1) * CW] = own_step(3, h, j).astype(BF16).reshape(NX, HT, CW)
        for r in (2, 1, 3):
            send(XS.at[j, xn(r)], XR.at[j, r - 1], xr + j * 3 + r - 1, {"x": xn(r)})
        total = XS[j, x].astype(F32)
        for r in (1, 3, 2):
            got(XR.at[j, r - 1], xr + j * 3 + r - 1)
            total = total + XR[j, r - 1].astype(F32)
        FO[j] = total.astype(BF16)
        for r in (2, 1, 3):
            send(FO.at[j], AG.at[r - 1, j], ag + j * 3 + r - 1, {"z": zn(r)})
        spread(FO.at[j], z, j, cc + j * 2)
    for j in range(2):
        for r in (1, 3, 2):
            got(AG.at[r - 1, j], ag + j * 3 + r - 1)
            spread(AG.at[r - 1, j], lax.rem(z + NZ - r, NZ), j, cc + 4 + (j * 3 + r - 1) * 2)

    for r in (1, 3, 2):
        got(JL.at[lax.rem(y + NY - r, NY)], jn + r - 1)
    sums = jnp.sum(JL[0] + JL[1] + JL[2] + JL[3], axis=1, keepdims=True)
    jl[...] = jnp.broadcast_to(sums / counts, (8, 128))

    for k in range(NK):
        for r in ORDER:
            cols = al(lax.rem(x + NX - r, NX) * U + k * CW, CW)
            got(lg.at[:, pl.ds(cols, CW)], lgs + k * 3 + r - 1)
    for r in ORDER:
        got(gr.at[:, pl.ds(al(lax.rem(x + NX - r, NX) * U, U), U)], grs + r - 1)
    for j in range(2):
        for h in range(2):
            rows = pl.ds(j * HT, HT)
            got(hg.at[rows, hg_cols(z, 1 - c, h)], cc + j * 2 + h)
            for r in (1, 3, 2):
                zz = lax.rem(z + NZ - r, NZ)
                got(hg.at[rows, hg_cols(zz, 1 - c, h)], cc + 4 + (j * 3 + r - 1) * 2 + h)

    def core_sent(i, carry):
        ps_copy(i).wait_send()
        return carry

    lax.fori_loop(0, 16, core_sent, 0)
    for s in range(3):
        for h in range(2):
            for j in range(2):
                ring_copy(s, h, j).wait_send()
    drain_sends(pending)
    drain(outs)
    assert used["s"] <= NSEND and used["r"] <= NRECV and used["l"] <= NLOAD, used


NSEND, NRECV, NLOAD = 192, 176, 88


def vmem(*shape, dtype=BF16):
    return pltpu.VMEM(shape, dtype)


def shards(hidden, weight, down, up, labels, jobs):
    pad = 3 * 128 - T
    lab = jnp.pad(labels.astype(F32), (0, pad)).reshape(3, 1, 128)
    job = jnp.pad(jobs.astype(F32), (0, pad), constant_values=-1.0).reshape(3, 1, 128)
    aux = jnp.concatenate([lab, job, jnp.zeros((3, 6, 128), F32)], axis=1)
    hbm = pl.BlockSpec(memory_space=pl.ANY)
    vm = pl.BlockSpec(memory_space=pltpu.VMEM)
    logits, rows, grad, loss, job_loss = pl.pallas_call(
        kernel,
        out_shape=(
            jax.ShapeDtypeStruct((T, V), BF16),
            jax.ShapeDtypeStruct((T, V), BF16),
            jax.ShapeDtypeStruct((T, D), BF16),
            jax.ShapeDtypeStruct((T, 128), F32),
            jax.ShapeDtypeStruct((8, 128), F32),
        ),
        in_specs=[hbm] * 5,
        out_specs=(hbm, hbm, hbm, vm, vm),
        scratch_shapes=[
            vmem(S, D),
            vmem(D, U + 256),
            vmem(DB, V),
            vmem(NK, S, CW, dtype=F32),
            vmem(S, U),
            vmem(NX, T, U + 256),
            vmem(16, S // 2, CW),
            vmem(12, S // 2, CW),
            vmem(4, S // 2, CW),
            vmem(2, NX, HT, SH),
            vmem(2, 3, HT, SH),
            vmem(2, HT, SH),
            vmem(3, 2, HT, SH),
            vmem(S, 128, dtype=F32),
            vmem(S, 128, dtype=F32),
            vmem(S, 128),
            vmem(128, U),
            vmem(NX, 3, 8, 128, dtype=F32),
            vmem(NZ * NC, NB, 8, 128, dtype=F32),
            vmem(NX, NB, 8, 128, dtype=F32),
            vmem(NB, 8, 128, dtype=F32),
            vmem(NY, 8, 128, dtype=F32),
            vmem(NY, 8, 128, dtype=F32),
            pltpu.SemaphoreType.DMA((NSEND,)),
            pltpu.SemaphoreType.DMA((NRECV,)),
            pltpu.SemaphoreType.DMA((NLOAD,)),
        ],
        compiler_params=pltpu.CompilerParams(
            collective_id=0, has_side_effects=True, vmem_limit_bytes=66 * 1024 * 1024 - 4 * 1024 * 1024
        ),
        name="step",
    )(hidden, weight, down, up, aux)
    return logits, rows, grad, loss[:, 3], job_loss[:, 0]


def solution(mesh):
    split = Mesh(mesh.devices.reshape(NZ, NC, NX, NY), ("z", "c", "x", "y"))
    dp, vocab = ("x", "y"), ("z", "c")
    return jax.shard_map(
        shards,
        mesh=split,
        in_specs=(P(dp, None), P(dp, vocab), P(), P(None, vocab), P(dp), P(dp)),
        out_specs=(P(dp, vocab), P(dp, vocab), P(dp, None), P(dp), P()),
        check_vma=False,
    )
```

time: 361 us -> 218 us (0.60)
  waiting for transfers between devices: 231 us -> 0 us
  Pallas kernels: 0 us -> 203 us
  matrix products: 54.7 us -> 0 us
  blocking collectives: 35.2 us -> 0 us
  between operations: 13.8 us -> 0.66 us
  other arithmetic: 14.4 us -> 2.04 us
  local copies, waits for them, and re-layouts: 5.36 us -> 11.5 us
  starting transfers between devices: 5.34 us -> 0 us
    pallas_call x0 -> x1, Pallas kernels: none -> 203 us  [shards(): pl.pallas_call(kernel, out_shape=(jax.ShapeDtypeStruct((T, V), BF16), jax...]
    all_gather x2 -> x0, waiting for transfers between devices: 196 us -> none  [the longest x1 182 us: shards(): lax.all_gather(output_projection_weight, DP, axis=0, tiled=True)]
    dot_general x5 -> x0, matrix products: 54.7 us -> none  [the longest x1 18.9 us: shards(): jnp.einsum('tv,dv->td', logit_gradient_rows, full_weight, preferred_eleme...]
    psum x4 -> x0, blocking collectives: 35.2 us -> none  [one_axis_at_a_time(): shard = lax.psum(shard, axis)]
    reduce_scatter x1 -> x0, waiting for transfers between devices: 30.4 us -> none  [shards(): lax.psum_scatter(grad_terms.astype(jnp.bfloat16), 'vocab', scatter_dimens...]
    convert_element_type x1 -> x2, other arithmetic: 7.79 us -> 1.37 us  [the longest x1 0.68 us: shards(): lab = jnp.pad(labels.astype(F32), (0, pad)).reshape(3, 1, 128)]
    reduce_sum x3 -> x0, other arithmetic: 5.3 us -> none  [the longest x1 4.25 us: shards(): jnp.sum(jnp.exp(complete_logit_rows - local_max[:, None]), axis=1)]
    all_to_all x1 -> x0, starting transfers between devices: 5.26 us -> none  [from_everyone(): lax.all_to_all(jnp.broadcast_to(shard[None], (count, *shard.shape)), axis...]
  transfers between devices with their start and end apart: 4 -> 0, of which waited for: 4 -> 0; matrix products, arithmetic and copies ran while one was open for 1% -> 0% of each run, Pallas kernels for 0% -> 0%
where the time goes in v1:
time: 218 us
  Pallas kernels  203 us (93%)
  local copies, waits for them, and re-layouts  11.5 us (5%)
    pallas_call x1, Pallas kernels, shards(): pl.pallas_call(kernel, out_shape=(jax.ShapeDtypeStruct((T, V), BF16), jax...  203 us
    unnamed x7, local copies, waits for them, and re-layouts  8.3 us

profile of v1, /device:TPU:1, one launch (start us, length us, event | category | flops | bytes accessed | tf_op | source)
XLA Modules:
  0.0 217.5 jit_solution(13603712181228205963)
XLA Ops:
  0.6 0.1 pad.12.clone
  0.7 0.7 convert_element_type.8
  1.4 0.7 convert_element_type.9
  2.1 0.7 maximum_maximum_fusion.aux
  2.8 203.4 %step.1 = (bf16[352,4096]{1,0:T(8,128)(2,1)}, bf16[352,4096]{1,0:T(8,128)(2,1)}, bf16[352,4096]{1,0:T(8,128)(2,1)}, f32[352,128]{1,0:T(8,128)}, f32[8,128]{1,0:T(8,128)}) custom-call(bf16[352,4096]{1,0:T(8,128)(2,1)} %hid.1, bf16[256,4096]{1,0:T(8,128)(2,1)} %w.1, bf16[4096,128]{1,0:T(8,128)(2,1)} %ad.1, bf16[128,4096]{1,0:T(8,128)(2,1)} %au.1, ...), custom_call_target="tpu_custom_call" | custom-call | tf_op jit(solution)/shard_map/step/pallas_call | solution.py:555
  206.2 1.3 slice_reduce_fusion.1
  207.5 1.7 slice_reduce_fusion
  209.2 0.0 copy-start.1
  209.2 3.9 %copy.14 = bf16[352,4096]{1,0:T(8,128)(2,1)} copy(bf16[352,4096]{1,0:T(8,128)(2,1)} %get-tuple-element.20) | data formatting | bytes 5767168
  213.1 0.0 copy-done.1
  213.1 0.0 copy-start
  213.1 1.6 copy.15
  214.7 1.3 copy-done
  216.0 1.6 copy.16
  (5 shorter events, 0.0 us)
Async XLA Ops:
  209.2 3.9 %copy-start.1 = (bf16[352,4096]{1,0:T(8,128)(2,1)S(1)}, bf16[352,4096]{1,0:T(8,128)(2,1)}, u32[]{:S(2)}) copy-start(bf16[352,4096]{1,0:T(8,128)(2,1)} %get-tuple-element.21) | copy-start | bytes 8650756
  213.1 2.9 %copy-start = (bf16[352,4096]{1,0:T(8,128)(2,1)S(1)}, bf16[352,4096]{1,0:T(8,128)(2,1)}, u32[]{:S(2)}) copy-start(bf16[352,4096]{1,0:T(8,128)(2,1)} %get-tuple-element.22) | copy-start | bytes 8650756

commit v2 on v1

--- a/solution.py
+++ b/solution.py
@@ -41,7 +41,7 @@
 def kernel(
     hid, w, ad, au, aux,
     lg, gr, hg, tl, jl,
-    H, W5, WS, E, LT, G5, RC, RR, R0, XS, XR, FO, AG, COL, COL2, LI, AU, AX, STA, STB, JR, CN, JL,
+    H, W5, WS, E, LT, G5, RR, R0, XS, XR, FO, AG, COL, COL2, LI, AU, AX, STA, STB, JR, CN, JL,
     ssem, rsem, lsem,
 ):
     z, c, x, y = (lax.axis_index(a) for a in ("z", "c", "x", "y"))
@@ -97,6 +97,16 @@
             d.wait_send()
         keep.clear()
 
+    scope = []
+
+    def phase(name):
+        if scope:
+            scope.pop().__exit__(None, None, None)
+        if name:
+            scope.append(jax.named_scope(name))
+            scope[0].__enter__()
+
+    phase("entry")
     bar = pltpu.get_barrier_semaphore()
     peers = (
         [{"x": xn(r)} for r in (1, 2, 3)]
@@ -129,9 +139,15 @@
     wx = take("r", NK * 3)
     hx = take("r", 3)
     ax = take("r", 3)
-    wy = take("r", NK * 4)
+    wy = take("r", NK * NX * 3)
     hz = take("r", 3 * 4)
     hc = take("r", 3 * 5)
+    lgs = take("r", NK * 3)
+    lgs_s = take("s", NK * 3)
+    lgs_l = take("l", NK)
+
+    def xp(r):
+        return lax.rem(x + NX - r, NX)
 
     def wblock(row, k):
         return W5.at[row, pl.ds(k * CW, CW)]
@@ -143,56 +159,53 @@
                 wblock(own_rows, k), wx + k * 3 + r - 1, {"x": xn(r)},
             )
 
-    drain(first)
-    send_w(0)
-    for r in ORDER:
-        send(AX.at[x], AX.at[x], ax + r - 1, {"x": xn(r)})
-    drain(own_h)
+    def piece(dy, r, k):
+        return wblock(pl.ds(al((yn(dy) * NX + xp(r)) * DB, DB), DB), k)
+
+    def y_own(k, r):
+        src = piece(0, r, k)
+        if r:
+            got(src, wx + k * 3 + r - 1)
+        at = wy + (k * NX + r) * 3
+        send(src, src, at, {"y": yn(1)})
+        send(src, src, at + 1, {"y": yn(3)})
+
+    def y_fwd(k, r):
+        at = wy + (k * NX + r) * 3
+        if r in (0, 2):
+            src = piece(3, r, k)
+            got(src, at)
+            send(src, src, at + 2, {"y": yn(1)})
+        else:
+            src = piece(1, r, k)
+            got(src, at + 1)
+            send(src, src, at + 2, {"y": yn(3)})
+
+    def w_end(k):
+        for r in (0, 1, 3, 2):
+            at = wy + (k * NX + r) * 3
+            if r in (0, 2):
+                got(piece(1, r, k), at + 1)
+            else:
+                got(piece(3, r, k), at)
+            got(piece(2, r, k), at + 2)
+
     hsends = []
+    other = {"c": 1 - c}
 
     def hpiece(xb, share, lo=0, n=T):
         return H.at[pl.ds(al(xb * T + lo, 16), n), pl.ds(al(share * SH, SH), SH)]
 
-    for r in ORDER:
-        send(hpiece(x, v), hpiece(x, v), hx + r - 1, {"x": xn(r)}, hsends)
-    for k in range(1, NK):
-        send_w(k)
-
-    def ysrc(dy, k, lo=0, n=NX * DB):
-        return wblock(pl.ds(al(yn(dy) * (NX * DB) + lo, DB), n), k)
-
-    HB = NX * DB // 2
-
-    def w_own(k):
-        for r in ORDER:
-            row = pl.ds(al((y * NX + lax.rem(x + NX - r, NX)) * DB, DB), DB)
-            got(wblock(row, k), wx + k * 3 + r - 1)
-        send(ysrc(0, k), ysrc(0, k), wy + k * 4 + 0, {"y": yn(1)})
-        send(ysrc(0, k), ysrc(0, k), wy + k * 4 + 1, {"y": yn(3)})
-
-    def w_fwd(k):
-        got(ysrc(3, k), wy + k * 4 + 0)
-        send(ysrc(3, k, 0, HB), ysrc(3, k, 0, HB), wy + k * 4 + 2, {"y": yn(1)})
-        got(ysrc(1, k), wy + k * 4 + 1)
-        send(ysrc(1, k, HB, HB), ysrc(1, k, HB, HB), wy + k * 4 + 3, {"y": yn(3)})
-
-    def w_end(k):
-        got(ysrc(2, k, 0, HB), wy + k * 4 + 2)
-        got(ysrc(2, k, HB, HB), wy + k * 4 + 3)
-
-    other = {"c": 1 - c}
-
     def h_in(r):
-        xb = lax.rem(x + NX - r, NX)
-        got(hpiece(xb, v), hx + r - 1)
-        mine = hpiece(xb, v)
+        mine = hpiece(xp(r), v)
+        got(mine, hx + r - 1)
         b = hz + (r - 1) * 4
         send(mine, mine, b + 0, {"z": zn(1)}, hsends)
         send(mine, mine, b + 1, {"z": zn(3)}, hsends)
         send(mine, mine, hc + (r - 1) * 5, other, hsends)
 
     def h_fwd(r):
-        xb = lax.rem(x + NX - r, NX)
+        xb = xp(r)
         b, d = hz + (r - 1) * 4, hc + (r - 1) * 5
         left, right = zn(3) * NC + c, zn(1) * NC + c
         got(hpiece(xb, left), b + 0)
@@ -203,7 +216,7 @@
         send(hpiece(xb, right), hpiece(xb, right), d + 2, other, hsends)
 
     def h_last(r):
-        xb = lax.rem(x + NX - r, NX)
+        xb = xp(r)
         b, d = hz + (r - 1) * 4, hc + (r - 1) * 5
         far = zn(2) * NC + c
         got(hpiece(xb, far, 0, HT), b + 2)
@@ -212,7 +225,7 @@
         send(hpiece(xb, far, HT, HT), hpiece(xb, far, HT, HT), d + 4, other, hsends)
 
     def h_end(r):
-        xb = lax.rem(x + NX - r, NX)
+        xb = xp(r)
         d = hc + (r - 1) * 5
         k = 1 - c
         got(hpiece(xb, v - c + k), d)
@@ -221,22 +234,101 @@
         got(hpiece(xb, zn(2) * NC + k, 0, HT), d + 3)
         got(hpiece(xb, zn(2) * NC + k, HT, HT), d + 4)
 
-    w_own(0)
+    lane128 = lax.broadcasted_iota(jnp.int32, (T, 128), 1)
+    rank_job = (lane128 // RANK).astype(F32)
+    base = v * V + x * U
+    lane_cw = lax.broadcasted_iota(jnp.int32, (T, CW), 1)
+    outs = []
+    my_cols = al(x * U, U)
+
+    def lora_in(r):
+        rows = pl.ds(al(xp(r) * T, 16), T)
+        hit = COL[rows, 1:2] == rank_job
+        a = fdot(H[rows, :], W5[:, U : U + 128])
+        LI[rows, :] = jnp.where(hit, a, 0.0).astype(BF16)
+
+    def lg_cols(k):
+        return pl.ds(al(my_cols + k * CW, CW), CW)
+
+    def lg_remote(k, r):
+        i = k * 3 + NX - 1 - r
+        src = LT.at[pl.ds(al(xp(r) * T, 16), T), pl.ds(al(k * CW, CW), CW)]
+        return rcopy(src, lg.at[:, lg_cols(k)], lgs_s + i, lgs + i, {"x": xp(r)})
+
+    def lg_local(k):
+        src = LT.at[pl.ds(al(x * T, 16), T), pl.ds(al(k * CW, CW), CW)]
+        return pltpu.make_async_copy(src, lg.at[:, lg_cols(k)], lsem.at[lgs_l + k])
+
+    def task(k, r):
+        rows = pl.ds(al(xp(r) * T, 16), T)
+        cols = pl.ds(al(k * CW, CW), CW)
+        a = fdot(H[rows, :], W5[:, cols])
+        a = a + fdot(LI[rows, :], AU[:, cols])
+        LT[rows, cols] = a.astype(BF16)
+        top = jnp.max(a, axis=1, keepdims=True)
+        e = jnp.exp(a - top)
+        E[k, rows, :] = e
+        total = jnp.sum(e, axis=1, keepdims=True)
+        ids = (lane_cw + (base + k * CW)).astype(F32)
+        target = jnp.sum(jnp.where(ids == COL[rows, 0:1], a, 0.0), axis=1, keepdims=True)
+        old = COL[rows, :]
+        old = jnp.where(lane128 == 8 + k, top, old)
+        old = jnp.where(lane128 == 12 + k, total, old)
+        COL[rows, :] = jnp.where(lane128 == 16 + k, target, old)
+
+    def tasks(k0, nk, o0, no):
+        def step(i, carry):
+            k, o = k0 + i // no, o0 + lax.rem(i, no)
+            r = jnp.where(o == 2, 3, jnp.where(o == 3, 2, o))
+            task(k, r)
+            if o0:
+                lg_remote(k, r).start()
+            else:
+                pl.when(r > 0)(lambda: lg_remote(k, r).start())
+                pl.when(r == 0)(lambda: lg_local(k).start())
+            return carry
+
+        lax.fori_loop(0, nk * no, step, 0)
+
+    drain(first)
+    send_w(0)
     for r in ORDER:
-        h_in(r)
-    w_own(1)
-    w_fwd(0)
-    h_fwd(1)
-    w_own(2)
-    h_fwd(3)
-    h_last(1)
-    w_fwd(1)
-    h_fwd(2)
-    h_last(3)
-    w_own(3)
-
+        send(AX.at[x], AX.at[x], ax + r - 1, {"x": xn(r)})
+    send_w(1)
+    for k in range(3):
+        y_own(k, 0)
+    drain(own_h)
     for r in ORDER:
-        got(AX.at[lax.rem(x + NX - r, NX)], ax + r - 1)
+        send(hpiece(x, v), hpiece(x, v), hx + r - 1, {"x": xn(r)}, hsends)
+    send_w(2)
+    send_w(3)
+    phase("p1a")
+    y_fwd(0, 0)
+    for r in ORDER:
+        y_own(0, r)
+    phase("p1b")
+    for r in ORDER:
+        y_own(1, r)
+    phase("p1c")
+    y_fwd(0, 1)
+    y_fwd(0, 3)
+    phase("h_in13")
+    h_in(1)
+    h_in(3)
+    phase("p1d")
+    y_fwd(0, 2)
+    y_own(3, 0)
+    y_fwd(1, 0)
+    y_fwd(1, 1)
+    phase("h_in2")
+    h_in(2)
+    phase("p1e")
+    y_fwd(1, 3)
+    y_fwd(1, 2)
+    phase("cols")
+
+    for r in ORDER:
+        got(AX.at[xp(r)], ax + r - 1)
     sub = lax.broadcasted_iota(jnp.int32, (8, 128), 0).astype(F32)
     subi = lax.broadcasted_iota(jnp.int32, (8, 128), 0)
     counts = jnp.zeros((8, 128), F32)
@@ -252,74 +344,68 @@
     for r in (1, 3, 2):
         send(CN.at[y], CN.at[y], cn + r - 1, {"y": yn(r)})
     drain(rest)
-    w_fwd(2)
+    lora_in(0)
+    phase("h_fwd1")
+    h_fwd(1)
+    phase("w_end0")
+    w_end(0)
+    phase("t0_0")
+    tasks(0, 1, 0, 1)
+    phase("y_own2")
+    for r in ORDER:
+        y_own(2, r)
+    phase("w_end1")
+    w_end(1)
+    phase("t1_0")
+    tasks(1, 1, 0, 1)
+    phase("h_fwd3")
+    h_fwd(3)
+    phase("y_own3")
+    for r in ORDER:
+        y_own(3, r)
+    phase("h_last1")
+    h_last(1)
+    phase("y_fwd2")
+    y_fwd(2, 0)
+    y_fwd(2, 1)
+    phase("h_fwd2")
+    h_fwd(2)
+    phase("h_end1")
+    h_end(1)
+    phase("t01_1")
+    lora_in(1)
+    tasks(0, 2, 1, 1)
+    phase("y_fwd2b")
+    y_fwd(2, 3)
+    y_fwd(2, 2)
+    phase("h_last3")
+    h_last(3)
+    h_end(3)
+    phase("t01_3")
+    lora_in(3)
+    tasks(0, 2, 2, 1)
+    phase("y_fwd3")
+    y_fwd(3, 0)
+    y_fwd(3, 1)
+    phase("w_end2")
+    w_end(2)
+    phase("t2")
+    tasks(2, 1, 0, 3)
+    phase("h_last2")
     h_last(2)
-    w_end(0)
-    for r in ORDER:
-        h_end(r)
+    h_end(2)
+    phase("t012_2")
+    lora_in(2)
+    tasks(0, 3, 3, 1)
+    phase("y_fwd3b")
+    y_fwd(3, 3)
+    y_fwd(3, 2)
     drain_sends(hsends)
-
-    lane128 = lax.broadcasted_iota(jnp.int32, (T, 128), 1)
-    rank_job = (lane128 // RANK).astype(F32)
-
-    def lora_in(m, carry):
-        rows = pl.ds(al(m * T, 16), T)
-        hit = COL[rows, 1:2] == rank_job
-        a = fdot(H[rows, :], W5[:, U : U + 128])
-        LI[rows, :] = jnp.where(hit, a, 0.0).astype(BF16)
-        return carry
-
-    lax.fori_loop(0, NX, lora_in, 0)
-
-    base = v * V + x * U
-    lane_cw = lax.broadcasted_iota(jnp.int32, (T, CW), 1)
-    lgs = take("r", NK * 3)
-    outs = []
-    my_cols = al(x * U, U)
-
-    def forward(k):
-        def step(m, carry):
-            rows = pl.ds(al(m * T, 16), T)
-            a = fdot(H[rows, :], W5[:, k * CW : (k + 1) * CW])
-            a = a + fdot(LI[rows, :], AU[:, k * CW : (k + 1) * CW])
-            LT[rows, k * CW : (k + 1) * CW] = a.astype(BF16)
-            top = jnp.max(a, axis=1, keepdims=True)
-            e = jnp.exp(a - top)
-            E[k, rows, :] = e
-            total = jnp.sum(e, axis=1, keepdims=True)
-            cols = (lane_cw + (base + k * CW)).astype(F32)
-            target = jnp.sum(jnp.where(cols == COL[rows, 0:1], a, 0.0), axis=1, keepdims=True)
-            old = COL[rows, :]
-            old = jnp.where(lane128 == 8 + k, top, old)
-            old = jnp.where(lane128 == 12 + k, total, old)
-            COL[rows, :] = jnp.where(lane128 == 16 + k, target, old)
-            return carry
-
-        lax.fori_loop(0, NX, step, 0)
-
-    def send_logits(k):
-        for r in ORDER:
-            send(
-                LT.at[pl.ds(al(xn(r) * T, 16), T), pl.ds(k * CW, CW)],
-                lg.at[:, pl.ds(al(my_cols + k * CW, CW), CW)],
-                lgs + k * 3 + r - 1, {"x": xn(r)},
-            )
-        load(
-            LT.at[pl.ds(al(x * T, 16), T), pl.ds(k * CW, CW)],
-            lg.at[:, pl.ds(al(my_cols + k * CW, CW), CW)], outs,
-        )
-
-    forward(0)
-    send_logits(0)
-    w_end(1)
-    forward(1)
-    send_logits(1)
-    w_fwd(3)
-    w_end(2)
-    forward(2)
-    send_logits(2)
+    phase("w_end3")
     w_end(3)
-    forward(3)
+    phase("t3")
+    tasks(3, 1, 0, 4)
+    phase("stats_a")
 
     def row_stats(b, carry):
         t = COL[pl.ds(al(b * 128, 128), 128), :].T
@@ -331,7 +417,7 @@
         STA[v, b] = jnp.where(subi == 0, top, jnp.where(subi == 1, s, jnp.where(subi == 2, g, 0.0)))
         return carry
 
-    lax.fori_loop(0, NB, row_stats, 0)
+    lax.fori_loop(0, NB, row_stats, 0, unroll=True)
     sa = take("r", 7)
     sb = take("r", 3)
     turns = [(a, b) for a in (2, 1, 3, 0) for b in range(NC) if a or b]
@@ -353,10 +439,10 @@
         STB[x, b] = jnp.where(subi == 0, top, jnp.where(subi == 1, s, jnp.where(subi == 2, g, 0.0)))
         return carry
 
-    lax.fori_loop(0, NB, stage_b, 0)
+    phase("stats_b")
+    lax.fori_loop(0, NB, stage_b, 0, unroll=True)
     for r in (2, 1, 3):
         send(STB.at[x], STB.at[x], sb + r - 1, {"x": xn(r)})
-    send_logits(3)
     for r in (1, 3, 2):
         got(CN.at[lax.rem(y + NY - r, NY)], cn + r - 1)
     counts = jnp.sum(CN[0] + CN[1] + CN[2] + CN[3], axis=1, keepdims=True)
@@ -378,33 +464,40 @@
         COL2[pl.ds(al(b * 128, 128), 128), :] = turned
         return job_sums + onehot * loss
 
-    JL[y] = lax.fori_loop(0, NB, finish, jnp.zeros((8, 128), F32))
+    phase("finish")
+    JL[y] = lax.fori_loop(0, NB, finish, jnp.zeros((8, 128), F32), unroll=True)
     jn = take("r", 3)
     for r in (1, 3, 2):
         send(JL.at[y], JL.at[y], jn + r - 1, {"y": yn(r)})
-    tl[...] = COL2[pl.ds(al(x * T, 8), T), :]
-
-    def gradient(m, carry):
-        rows = pl.ds(al(m * T, 16), T)
-        lab = COL[rows, 0:1]
-        weight = COL2[rows, 2:3]
-        for k in range(NK):
-            f = jnp.exp(COL[rows, 8 + k : 9 + k] - COL2[rows, 0:1]) * COL2[rows, 1:2]
-            cols = (lane_cw + (base + k * CW)).astype(F32)
-            g = E[k, rows, :] * f - jnp.where(cols == lab, weight, 0.0)
-            G5[m, :, k * CW : (k + 1) * CW] = g.astype(BF16)
-        part = tdot(G5[m, :, 0:U], AU[...])
-        part = jnp.where(COL[rows, 1:2] == rank_job, part, 0.0)
-        high = part.astype(BF16)
-        G5[m, :, U : U + 128] = high
-        G5[m, :, U + 128 : U + 256] = (part - high.astype(F32)).astype(BF16)
-        return carry
-
-    lax.fori_loop(0, NX, gradient, 0)
-    grs = take("r", 3)
-    for r in ORDER:
-        send(G5.at[xn(r), :, pl.ds(0, U)], gr.at[:, pl.ds(my_cols, U)], grs + r - 1, {"x": xn(r)})
-    load(G5.at[x, :, pl.ds(0, U)], gr.at[:, pl.ds(my_cols, U)], outs)
+
+    grs = take("r", 6)
+
+    def gradient(j):
+        def step(m, carry):
+            half = pl.ds(j * HT, HT)
+            rows = pl.ds(al(m * T + j * HT, 16), HT)
+            lab = COL[rows, 0:1]
+            weight = COL2[rows, 2:3]
+            for k in range(NK):
+                f = jnp.exp(COL[rows, 8 + k : 9 + k] - COL2[rows, 0:1]) * COL2[rows, 1:2]
+                ids = (lane_cw[:HT] + (base + k * CW)).astype(F32)
+                g = E[k, rows, :] * f - jnp.where(ids == lab, weight, 0.0)
+                G5[m, half, k * CW : (k + 1) * CW] = g.astype(BF16)
+            part = tdot(G5[m, half, 0:U], AU[...])
+            part = jnp.where(COL[rows, 1:2] == rank_job[:HT], part, 0.0)
+            high = part.astype(BF16)
+            G5[m, half, U : U + 128] = high
+            G5[m, half, U + 128 : U + 256] = (part - high.astype(F32)).astype(BF16)
+            return carry
+
+        lax.fori_loop(0, NX, step, 0)
+
+    def send_rows(j):
+        half = pl.ds(j * HT, HT)
+        dst = gr.at[half, pl.ds(my_cols, U)]
+        for r in ORDER:
+            send(G5.at[xn(r), half, pl.ds(0, U)], dst, grs + j * 3 + r - 1, {"x": xn(r)})
+        load(G5.at[x, half, pl.ds(0, U)], dst, outs)
 
     cs_s, cs_r = take("s", 16), take("r", 16)
     ring_s, ring_r = take("s", 12), take("r", 12)
@@ -420,18 +513,22 @@
     def ps(i):
         return H.at[pl.ds(al(lax.rem(i, 2) * (S // 2), 16), S // 2), pl.ds(al(i // 2 * CW, CW), CW)]
 
+    def rc(i):
+        cols = pl.ds(al(D // 2 + i // 2 * CW, CW), CW)
+        return H.at[pl.ds(al(lax.rem(i, 2) * (S // 2), 16), S // 2), cols]
+
     def ps_copy(i):
-        return rcopy(ps(i), RC.at[i], cs_s + i, cs_r + i, other)
-
-    def for_core(s):
+        return rcopy(ps(i), rc(i), cs_s + i, cs_r + i, other)
+
+    def for_core(s, j0=0, nj=2):
         def step(q, carry):
-            j, h = q // 2, lax.rem(q, 2)
+            j, h = j0 + q // 2, lax.rem(q, 2)
             i = s * 4 + h * 2 + j
             ps(i)[...] = unit(s, h, j, 1 - c).astype(BF16)
             ps_copy(i).start()
             return carry
 
-        lax.fori_loop(0, 4, step, 0)
+        lax.fori_loop(0, 2 * nj, step, 0)
 
     def ring_copy(s, h, j):
         i = h * 2 + j
@@ -445,15 +542,15 @@
         i = h * 2 + j
         a = unit(s, h, j, c)
         ps_copy(s * 4 + i).wait_recv()
-        a = a + RC[s * 4 + i].astype(F32)
+        a = a + rc(s * 4 + i)[...].astype(F32)
         if s:
             ring_copy(s - 1, h, j).wait_recv()
             a = a + RR[(s - 1) * 4 + i].astype(F32)
         return a
 
-    def own(s):
+    def own(s, j0=0, nj=2):
         def step(q, carry):
-            j, h = q // 2, lax.rem(q, 2)
+            j, h = j0 + q // 2, lax.rem(q, 2)
             i = h * 2 + j
             a = own_step(s, h, j).astype(BF16)
             if s == 0:
@@ -463,15 +560,33 @@
             ring_copy(s, h, j).start()
             return carry
 
-        lax.fori_loop(0, 4, step, 0)
-
-    for_core(0)
+        lax.fori_loop(0, 2 * nj, step, 0)
+
+    phase("grad0")
+    gradient(0)
+    phase("core00")
+    for_core(0, 0, 1)
+    send_rows(0)
+    tl[...] = COL2[pl.ds(al(x * T, 8), T), :]
+    phase("own00")
+    own(0, 0, 1)
+    phase("grad1")
+    gradient(1)
+    phase("core01")
+    for_core(0, 1, 1)
+    send_rows(1)
+    phase("own01")
+    own(0, 1, 1)
+    phase("core1")
     for_core(1)
-    own(0)
+    phase("own1")
+    own(1)
+    phase("core2")
     for_core(2)
-    own(1)
+    phase("own2")
+    own(2)
+    phase("core3")
     for_core(3)
-    own(2)
 
     xr = take("r", 6)
     ag = take("r", 6)
@@ -488,8 +603,10 @@
             load(piece, dst, outs)
 
     for j in range(2):
+        phase("own3")
         for h in range(2):
             XS[j, :, :, h * CW : (h + 1) * CW] = own_step(3, h, j).astype(BF16).reshape(NX, HT, CW)
+        phase("xsum")
         for r in (2, 1, 3):
             send(XS.at[j, xn(r)], XR.at[j, r - 1], xr + j * 3 + r - 1, {"x": xn(r)})
         total = XS[j, x].astype(F32)
@@ -497,9 +614,11 @@
             got(XR.at[j, r - 1], xr + j * 3 + r - 1)
             total = total + XR[j, r - 1].astype(F32)
         FO[j] = total.astype(BF16)
+        phase("spread")
         for r in (2, 1, 3):
             send(FO.at[j], AG.at[r - 1, j], ag + j * 3 + r - 1, {"z": zn(r)})
         spread(FO.at[j], z, j, cc + j * 2)
+    phase("gathered")
     for j in range(2):
         for r in (1, 3, 2):
             got(AG.at[r - 1, j], ag + j * 3 + r - 1)
@@ -510,12 +629,17 @@
     sums = jnp.sum(JL[0] + JL[1] + JL[2] + JL[3], axis=1, keepdims=True)
     jl[...] = jnp.broadcast_to(sums / counts, (8, 128))
 
+    phase("arrivals")
     for k in range(NK):
         for r in ORDER:
-            cols = al(lax.rem(x + NX - r, NX) * U + k * CW, CW)
+            cols = al(xp(r) * U + k * CW, CW)
             got(lg.at[:, pl.ds(cols, CW)], lgs + k * 3 + r - 1)
-    for r in ORDER:
-        got(gr.at[:, pl.ds(al(lax.rem(x + NX - r, NX) * U, U), U)], grs + r - 1)
+            lg_remote(k, r).wait_send()
+        lg_local(k).wait()
+    for j in range(2):
+        for r in ORDER:
+            cols = pl.ds(al(xp(r) * U, U), U)
+            got(gr.at[pl.ds(j * HT, HT), cols], grs + j * 3 + r - 1)
     for j in range(2):
         for h in range(2):
             rows = pl.ds(j * HT, HT)
@@ -533,12 +657,14 @@
         for h in range(2):
             for j in range(2):
                 ring_copy(s, h, j).wait_send()
+    phase("drain")
     drain_sends(pending)
     drain(outs)
+    phase(None)
     assert used["s"] <= NSEND and used["r"] <= NRECV and used["l"] <= NLOAD, used
 
 
-NSEND, NRECV, NLOAD = 192, 176, 88
+NSEND, NRECV, NLOAD = 224, 208, 88
 
 
 def vmem(*shape, dtype=BF16):
@@ -570,7 +696,6 @@
             vmem(NK, S, CW, dtype=F32),
             vmem(S, U),
             vmem(NX, T, U + 256),
-            vmem(16, S // 2, CW),
             vmem(12, S // 2, CW),
             vmem(4, S // 2, CW),
             vmem(2, NX, HT, SH),
@@ -592,7 +717,7 @@
             pltpu.SemaphoreType.DMA((NLOAD,)),
         ],
         compiler_params=pltpu.CompilerParams(
-            collective_id=0, has_side_effects=True, vmem_limit_bytes=66 * 1024 * 1024 - 4 * 1024 * 1024
+            collective_id=0, has_side_effects=True, vmem_limit_bytes=56 * 1024 * 1024
         ),
         name="step",
     )(hidden, weight, down, up, aux)

time: 218 us -> 206 us (0.945)
  Pallas kernels: 203 us -> 191 us
    pallas_call x1, Pallas kernels: 203 us -> 191 us  [shards(): pl.pallas_call(kernel, out_shape=(jax.ShapeDtypeStruct((T, V), BF16), jax...]
where the time goes in v2:
time: 206 us; the launch traced here: 205 us
  Pallas kernels  191 us (93%)
  local copies, waits for them, and re-layouts  11.5 us (6%)
    pallas_call x1, Pallas kernels, shards(): pl.pallas_call(kernel, out_shape=(jax.ShapeDtypeStruct((T, V), BF16), jax...  191 us
    unnamed x7, local copies, waits for them, and re-layouts  8.3 us

profile of v2, /device:TPU:1, one launch (start us, length us, event | category | flops | bytes accessed | tf_op | source)
XLA Modules:
  0.0 205.5 jit_solution(14684031583308025329)
XLA Ops:
  0.6 0.1 pad.12.clone
  0.7 0.7 convert_element_type.8
  1.4 0.7 convert_element_type.9
  2.1 0.7 maximum_maximum_fusion.aux
  2.8 191.3 %step.1 = (bf16[352,4096]{1,0:T(8,128)(2,1)}, bf16[352,4096]{1,0:T(8,128)(2,1)}, bf16[352,4096]{1,0:T(8,128)(2,1)}, f32[352,128]{1,0:T(8,128)}, f32[8,128]{1,0:T(8,128)}) custom-call(bf16[352,4096]{1,0:T(8,128)(2,1)} %hid.1, bf16[256,4096]{1,0:T(8,128)(2,1)} %w.1, bf16[4096,128]{1,0:T(8,128)(2,1)} %ad.1, bf16[128,4096]{1,0:T(8,128)(2,1)} %au.1, ...), custom_call_target="tpu_custom_call" | custom-call | tf_op jit(solution)/shard_map/step/pallas_call | solution.py:681
  194.2 1.3 slice_reduce_fusion.1
  195.5 1.7 slice_reduce_fusion
  197.2 0.0 copy-start.1
  197.2 3.9 %copy.14 = bf16[352,4096]{1,0:T(8,128)(2,1)} copy(bf16[352,4096]{1,0:T(8,128)(2,1)} %get-tuple-element.20) | data formatting | bytes 5767168
  201.1 0.0 copy-done.1
  201.1 0.0 copy-start
  201.1 1.6 copy.15
  202.6 1.3 copy-done
  203.9 1.6 copy.16
  (5 shorter events, 0.0 us)
Async XLA Ops:
  197.2 3.9 %copy-start.1 = (bf16[352,4096]{1,0:T(8,128)(2,1)S(1)}, bf16[352,4096]{1,0:T(8,128)(2,1)}, u32[]{:S(2)}) copy-start(bf16[352,4096]{1,0:T(8,128)(2,1)} %get-tuple-element.21) | copy-start | bytes 8650756
  201.1 2.9 %copy-start = (bf16[352,4096]{1,0:T(8,128)(2,1)S(1)}, bf16[352,4096]{1,0:T(8,128)(2,1)}, u32[]{:S(2)}) copy-start(bf16[352,4096]{1,0:T(8,128)(2,1)} %get-tuple-element.22) | copy-start | bytes 8650756

commit v3 on v2

v3 whole, which is shorter than its diff:
```python
import functools

import jax
import jax.numpy as jnp
from jax import lax
from jax.experimental import pallas as pl
from jax.experimental.pallas import tpu as pltpu
from jax.sharding import Mesh
from jax.sharding import PartitionSpec as P

MESH = pl.DeviceIdType.MESH
F32 = jnp.float32
BF16 = jnp.bfloat16

JOBS = 8
RANK = 16
NX = NY = NZ = 4
NC = 2
T = 352
S = NX * T
HT = T // 2
LEN = (96, 96, 80, 80)
OFF = (0, 96, 192, 272)
NQ = len(LEN)
D = 4096
DB = D // (NX * NY)
V = 4096
U = V // NX
CW = 256
NK = U // CW
SH = D // (NZ * NC)
TOKENS = S * NY
NB = S // 128


def fdot(a, b):
    return jnp.dot(a, b, preferred_element_type=F32)


def tdot(a, b):
    return lax.dot_general(a, b, (((1,), (1,)), ((), ())), preferred_element_type=F32)


def kernel(
    hid, w, ad, au, ids_in,
    lg, gr, hg, small,
    H, W5, WS, E, LT, G5, RR, XS, XR, FO, AG, COL, COL2, LI, AU, AX, STA, STB, JR, CN, JL,
    ssem, rsem, lsem,
):
    z, c, x, y = (lax.axis_index(a) for a in ("z", "c", "x", "y"))
    v = z * NC + c

    def al(i, m):
        return pl.multiple_of(i, m)

    def xn(r):
        return lax.rem(x + r, NX)

    def yn(r):
        return lax.rem(y + r, NY)

    def zn(r):
        return lax.rem(z + r, NZ)

    used = {"s": 0, "r": 0, "l": 0}

    def take(kind, n=1):
        at = used[kind]
        used[kind] = at + n
        return at

    pending = []

    def rcopy(src, dst, si, ri, dev):
        return pltpu.make_async_remote_copy(
            src_ref=src, dst_ref=dst, send_sem=ssem.at[si], recv_sem=rsem.at[ri],
            device_id=dev, device_id_type=MESH,
        )

    def send(src, dst, ri, dev, keep=pending):
        d = rcopy(src, dst, take("s"), ri, dev)
        d.start()
        keep.append(d)

    def got(dst, ri):
        rcopy(dst, dst, 0, ri, {"x": xn(1)}).wait_recv()

    def load(src, dst, keep):
        d = pltpu.make_async_copy(src, dst, lsem.at[take("l")])
        d.start()
        keep.append(d)

    def drain(keep):
        for d in keep:
            d.wait()
        keep.clear()

    def drain_sends(keep):
        for d in keep:
            d.wait_send()
        keep.clear()

    scope = []

    def phase(name):
        if scope:
            scope.pop().__exit__(None, None, None)
        if name:
            scope.append(jax.named_scope(name))
            scope[0].__enter__()

    phase("entry")
    bar = pltpu.get_barrier_semaphore()
    peers = (
        [{"x": xn(r)} for r in (1, 2, 3)]
        + [{"y": yn(r)} for r in (1, 2, 3)]
        + [{"z": zn(a), "c": lax.rem(c + b, NC)} for a in range(NZ) for b in range(NC) if a or b]
    )
    for dev in peers:
        pl.semaphore_signal(bar, inc=1, device_id=dev, device_id_type=MESH)

    first, own_h, rest = [], [], []
    load(w, WS, first)
    for p in range(NX * NY):
        n = (p % NX) * NY + p // NX
        load(hid.at[:, pl.ds(n * DB, DB)], H.at[pl.ds(al(x * T, 16), T), pl.ds(p * DB, DB)], own_h)
    for q in range(3):
        n = min(128, T - q * 128)
        AX[x, q] = jnp.full((8, 128), -1.0, F32)
        AX[x, q, 0:2, 0:n] = ids_in[:, q * 128 : q * 128 + n].astype(F32)
    own_rows = pl.ds(al((y * NX + x) * DB, DB), DB)
    load(w.at[:, pl.ds(al(x * U, U), U)], W5.at[own_rows, pl.ds(0, U)], first)
    load(au.at[:, pl.ds(al(x * U, U), U)], AU, rest)
    for p in range(NX * NY):
        n = (p % NX) * NY + p // NX
        for q in range(2):
            load(
                ad.at[pl.ds(n * DB, DB), :],
                W5.at[pl.ds(p * DB, DB), pl.ds(U + q * 128, 128)],
                rest,
            )
    pl.semaphore_wait(bar, len(peers))

    ORDER = (1, 3, 2)
    wx = take("r", NK * 3)
    hx = take("r", 3)
    ax = take("r", 3)
    wy = take("r", NK * NX * 3)
    hz = take("r", 3 * 4)
    hc = take("r", 3 * 5)
    lgs = take("r", NK * 3)
    lgs_s = take("s", NK * 3)
    lgs_l = take("l", NK)

    def xp(r):
        return lax.rem(x + NX - r, NX)

    def wblock(row, k):
        return W5.at[row, pl.ds(k * CW, CW)]

    def send_w(k):
        for r in ORDER:
            send(
                WS.at[:, pl.ds(al(xn(r) * U + k * CW, CW), CW)],
                wblock(own_rows, k), wx + k * 3 + r - 1, {"x": xn(r)},
            )

    def piece(dy, r, k):
        return wblock(pl.ds(al((yn(dy) * NX + xp(r)) * DB, DB), DB), k)

    def y_own(k, r):
        src = piece(0, r, k)
        if r:
            got(src, wx + k * 3 + r - 1)
        at = wy + (k * NX + r) * 3
        send(src, src, at, {"y": yn(1)})
        send(src, src, at + 1, {"y": yn(3)})

    def y_fwd(k, r):
        at = wy + (k * NX + r) * 3
        if r in (0, 2):
            src = piece(3, r, k)
            got(src, at)
            send(src, src, at + 2, {"y": yn(1)})
        else:
            src = piece(1, r, k)
            got(src, at + 1)
            send(src, src, at + 2, {"y": yn(3)})

    def w_end(k):
        for r in (0, 1, 3, 2):
            at = wy + (k * NX + r) * 3
            if r in (0, 2):
                got(piece(1, r, k), at + 1)
            else:
                got(piece(3, r, k), at)
            got(piece(2, r, k), at + 2)

    hsends = []
    other = {"c": 1 - c}

    def hpiece(xb, share, lo=0, n=T):
        return H.at[pl.ds(al(xb * T + lo, 16), n), pl.ds(al(share * SH, SH), SH)]

    def h_in(r):
        mine = hpiece(xp(r), v)
        got(mine, hx + r - 1)
        b = hz + (r - 1) * 4
        send(mine, mine, b + 0, {"z": zn(1)}, hsends)
        send(mine, mine, b + 1, {"z": zn(3)}, hsends)
        send(mine, mine, hc + (r - 1) * 5, other, hsends)

    def h_fwd(r):
        xb = xp(r)
        b, d = hz + (r - 1) * 4, hc + (r - 1) * 5
        left, right = zn(3) * NC + c, zn(1) * NC + c
        got(hpiece(xb, left), b + 0)
        send(hpiece(xb, left, 0, HT), hpiece(xb, left, 0, HT), b + 2, {"z": zn(1)}, hsends)
        send(hpiece(xb, left), hpiece(xb, left), d + 1, other, hsends)
        got(hpiece(xb, right), b + 1)
        send(hpiece(xb, right, HT, HT), hpiece(xb, right, HT, HT), b + 3, {"z": zn(3)}, hsends)
        send(hpiece(xb, right), hpiece(xb, right), d + 2, other, hsends)

    def h_last(r):
        xb = xp(r)
        b, d = hz + (r - 1) * 4, hc + (r - 1) * 5
        far = zn(2) * NC + c
        got(hpiece(xb, far, 0, HT), b + 2)
        send(hpiece(xb, far, 0, HT), hpiece(xb, far, 0, HT), d + 3, other, hsends)
        got(hpiece(xb, far, HT, HT), b + 3)
        send(hpiece(xb, far, HT, HT), hpiece(xb, far, HT, HT), d + 4, other, hsends)

    def h_end(r):
        xb = xp(r)
        d = hc + (r - 1) * 5
        k = 1 - c
        got(hpiece(xb, v - c + k), d)
        got(hpiece(xb, zn(3) * NC + k), d + 1)
        got(hpiece(xb, zn(1) * NC + k), d + 2)
        got(hpiece(xb, zn(2) * NC + k, 0, HT), d + 3)
        got(hpiece(xb, zn(2) * NC + k, HT, HT), d + 4)

    lane128 = lax.broadcasted_iota(jnp.int32, (T, 128), 1)
    rank_job = (lane128 // RANK).astype(F32)
    base = v * V + x * U
    lane_cw = lax.broadcasted_iota(jnp.int32, (T, CW), 1)
    outs = []
    my_cols = al(x * U, U)

    def lora_in(r):
        rows = pl.ds(al(xp(r) * T, 16), T)
        hit = COL[rows, 1:2] == rank_job
        a = fdot(H[rows, :], W5[:, U : U + 128])
        LI[rows, :] = jnp.where(hit, a, 0.0).astype(BF16)

    def lg_cols(k):
        return pl.ds(al(my_cols + k * CW, CW), CW)

    def lg_remote(k, r):
        i = k * 3 + NX - 1 - r
        src = LT.at[pl.ds(al(xp(r) * T, 16), T), pl.ds(al(k * CW, CW), CW)]
        return rcopy(src, lg.at[:, lg_cols(k)], lgs_s + i, lgs + i, {"x": xp(r)})

    def lg_local(k):
        src = LT.at[pl.ds(al(x * T, 16), T), pl.ds(al(k * CW, CW), CW)]
        return pltpu.make_async_copy(src, lg.at[:, lg_cols(k)], lsem.at[lgs_l + k])

    def task(k, r):
        rows = pl.ds(al(xp(r) * T, 16), T)
        cols = pl.ds(al(k * CW, CW), CW)
        a = fdot(H[rows, :], W5[:, cols])
        a = a + fdot(LI[rows, :], AU[:, cols])
        LT[rows, cols] = a.astype(BF16)
        top = jnp.max(a, axis=1, keepdims=True)
        e = jnp.exp(a - top)
        E[k, rows, :] = e
        total = jnp.sum(e, axis=1, keepdims=True)
        ids = (lane_cw + (base + k * CW)).astype(F32)
        target = jnp.sum(jnp.where(ids == COL[rows, 0:1], a, 0.0), axis=1, keepdims=True)
        old = COL[rows, :]
        old = jnp.where(lane128 == 8 + k, top, old)
        old = jnp.where(lane128 == 12 + k, total, old)
        COL[rows, :] = jnp.where(lane128 == 16 + k, target, old)

    def tasks(k0, nk, o0, no, out=True):
        def step(i, carry):
            k, o = k0 + i // no, o0 + lax.rem(i, no)
            r = jnp.where(o == 2, 3, jnp.where(o == 3, 2, o))
            task(k, r)
            if not out:
                return carry
            if o0:
                lg_remote(k, r).start()
            else:
                pl.when(r > 0)(lambda: lg_remote(k, r).start())
                pl.when(r == 0)(lambda: lg_local(k).start())
            return carry

        lax.fori_loop(0, nk * no, step, 0)

    drain(first)
    send_w(0)
    for r in ORDER:
        send(AX.at[x], AX.at[x], ax + r - 1, {"x": xn(r)})
    send_w(1)
    for k in range(3):
        y_own(k, 0)
    drain(own_h)
    for r in ORDER:
        send(hpiece(x, v), hpiece(x, v), hx + r - 1, {"x": xn(r)}, hsends)
    send_w(2)
    send_w(3)
    phase("p1a")
    y_fwd(0, 0)
    for r in ORDER:
        y_own(0, r)
    phase("p1b")
    for r in ORDER:
        y_own(1, r)
    phase("p1c")
    y_fwd(0, 1)
    y_fwd(0, 3)
    phase("h_in13")
    h_in(1)
    h_in(3)
    phase("p1d")
    y_fwd(0, 2)
    y_own(3, 0)
    y_fwd(1, 0)
    y_fwd(1, 1)
    phase("cols")

    for r in ORDER:
        got(AX.at[xp(r)], ax + r - 1)
    sub = lax.broadcasted_iota(jnp.int32, (8, 128), 0).astype(F32)
    counts = jnp.zeros((8, 128), F32)
    for xb in range(NX):
        for q in range(3):
            tile = AX[xb, q]
            n = min(128, T - q * 128)
            turned = jnp.concatenate([tile, jnp.zeros((120, 128), F32)], axis=0).T
            COL[pl.ds(xb * T + q * 128, n), :] = turned[:n]
            counts = counts + (tile[1:2, :] == sub).astype(F32)
    CN[y] = counts
    cn = take("r", 3)
    for r in (1, 3, 2):
        send(CN.at[y], CN.at[y], cn + r - 1, {"y": yn(r)})
    drain(rest)
    lora_in(0)
    phase("p1e")
    y_fwd(1, 3)
    y_fwd(1, 2)
    phase("h_fwd1")
    h_fwd(1)
    phase("h_in2")
    h_in(2)
    phase("w_end0")
    w_end(0)
    phase("t0_0")
    tasks(0, 1, 0, 1)
    phase("y_own2")
    for r in ORDER:
        y_own(2, r)
    phase("h_fwd3")
    h_fwd(3)
    phase("y_own3")
    for r in ORDER:
        y_own(3, r)
    phase("w_end1")
    w_end(1)
    phase("t1_0")
    tasks(1, 1, 0, 1)
    phase("h_last1")
    h_last(1)
    h_end(1)
    phase("t01_1")
    lora_in(1)
    tasks(0, 2, 1, 1)
    phase("y_fwd2")
    for r in (0, 1, 3, 2):
        y_fwd(2, r)
    phase("h_fwd2")
    h_fwd(2)
    phase("h_last3")
    h_last(3)
    phase("y_fwd3")
    y_fwd(3, 0)
    y_fwd(3, 1)
    phase("h_end3")
    h_end(3)
    phase("t01_3")
    lora_in(3)
    tasks(0, 2, 2, 1)
    phase("y_fwd3b")
    y_fwd(3, 3)
    y_fwd(3, 2)
    phase("h_last2")
    h_last(2)
    h_end(2)
    phase("t01_2")
    lora_in(2)
    tasks(0, 2, 3, 1)
    drain_sends(hsends)
    phase("w_end2")
    w_end(2)
    phase("t2")
    tasks(2, 1, 0, 4)
    phase("w_end3")
    w_end(3)
    phase("t3")
    tasks(3, 1, 0, 4, False)
    phase("stats_a")

    STA[v] = jnp.broadcast_to(jnp.ones((1, 1, 1), F32), (3, 16, 128))
    JR[...] = jnp.full((16, 128), -1.0, F32)
    for b in range(NB):
        t = COL[b * 128 : (b + 1) * 128, :].T
        m, e, g = t[8:12], t[12:16], t[16:20]
        top = jnp.max(m, axis=0, keepdims=True)
        STA[v, 0, b : b + 1, :] = top
        STA[v, 1, b : b + 1, :] = jnp.sum(e * jnp.exp(m - top), axis=0, keepdims=True)
        STA[v, 2, b : b + 1, :] = jnp.sum(g, axis=0, keepdims=True)
        JR[b : b + 1, :] = t[1:2]
    sa = take("r", 7)
    sb = take("r", 3)
    turns = [(a, b) for a in (2, 1, 3, 0) for b in range(NC) if a or b]
    for a, b in turns:
        dev = {"z": zn(a), "c": lax.rem(c + b, NC)}
        send(STA.at[v], STA.at[v], sa + a * NC + b - 1, dev)
    phase("counts")
    for r in (1, 3, 2):
        got(CN.at[lax.rem(y + NY - r, NY)], cn + r - 1)
    counts = jnp.sum(CN[0] + CN[1] + CN[2] + CN[3], axis=1, keepdims=True)
    counts = jnp.maximum(counts, 1.0)
    per_job = TOKENS / (JOBS * counts)
    jobs = JR[...]
    weight = jnp.zeros((16, 128), F32)
    for j in range(JOBS):
        weight = jnp.where(jobs == float(j), per_job[j : j + 1, :], weight)
    phase("stats_w")
    for a, b in turns:
        src = lax.rem(z + NZ - a, NZ) * NC + lax.rem(c + b, NC)
        got(STA.at[src], sa + a * NC + b - 1)

    def joined(ref, n):
        top = functools.reduce(jnp.maximum, [ref[i, 0] for i in range(n)])
        e = functools.reduce(jnp.add, [ref[i, 1] * jnp.exp(ref[i, 0] - top) for i in range(n)])
        return top, e, functools.reduce(jnp.add, [ref[i, 2] for i in range(n)])

    STB[x, 0], STB[x, 1], STB[x, 2] = joined(STA, NZ * NC)
    phase("stats_b")
    for r in (2, 1, 3):
        send(STB.at[x], STB.at[x], sb + r - 1, {"x": xn(r)})
    for r in ORDER:
        lg_remote(NK - 1, r).start()
    lg_local(NK - 1).start()
    for r in (2, 1, 3):
        got(STB.at[xp(r)], sb + r - 1)
    phase("finish")
    top, e, g = joined(STB, NX)
    loss = top + jnp.log(e) - g
    scaled = weight / e
    blank = jnp.zeros((124, 128), F32)
    for b in range(NB):
        parts = [i[b : b + 1] for i in (top, scaled, weight, loss)]
        COL2[b * 128 : (b + 1) * 128, :] = jnp.concatenate(parts + [blank], axis=0).T

    grs = take("r", 6)

    def gradient(j):
        part = pl.ds(OFF[j], LEN[j])

        def step(m, carry):
            rows = pl.ds(al(m * T + OFF[j], 16), LEN[j])
            lab = COL[rows, 0:1]
            weight = COL2[rows, 2:3]
            for k in range(NK):
                f = jnp.exp(COL[rows, 8 + k : 9 + k] - COL2[rows, 0:1]) * COL2[rows, 1:2]
                ids = (lane_cw[: LEN[j]] + (base + k * CW)).astype(F32)
                g = E[k, rows, :] * f - jnp.where(ids == lab, weight, 0.0)
                G5[m, part, k * CW : (k + 1) * CW] = g.astype(BF16)
            lora = tdot(G5[m, part, 0:U], AU[...])
            lora = jnp.where(COL[rows, 1:2] == rank_job[: LEN[j]], lora, 0.0)
            high = lora.astype(BF16)
            G5[m, part, U : U + 128] = high
            G5[m, part, U + 128 : U + 256] = (lora - high.astype(F32)).astype(BF16)
            return carry

        lax.fori_loop(0, NX, step, 0)

    def send_rows(i):
        part = pl.ds(OFF[2 * i], LEN[2 * i] * 2)
        dst = gr.at[part, pl.ds(my_cols, U)]
        for r in ORDER:
            send(G5.at[xn(r), part, pl.ds(0, U)], dst, grs + i * 3 + r - 1, {"x": xn(r)})
        load(G5.at[x, part, pl.ds(0, U)], dst, outs)

    cs_s, cs_r = take("s", 32), take("r", 32)
    ring_s, ring_r = take("s", 24), take("r", 24)

    def zt(s, h):
        return lax.rem(z + NZ + (2 * h - 1) * (s + 1), NZ)

    def span(j):
        return pl.ds(NX * OFF[j], NX * LEN[j])

    def unit(s, h, j, core):
        at = al((zt(s, h) * NC + core) * SH + h * CW, CW)
        g = G5[:, OFF[j] : OFF[j] + LEN[j], :].reshape(NX * LEN[j], U + 256)
        return tdot(g, W5[pl.ds(at, CW), :])

    def ps(s, h, j, at=0):
        return H.at[span(j), pl.ds(al(at + (s * 2 + h) * CW, CW), CW)]

    def ps_copy(s, h, j):
        i = (s * 2 + h) * NQ + j
        return rcopy(ps(s, h, j), ps(s, h, j, D // 2), cs_s + i, cs_r + i, other)

    def ring_copy(s, h, j):
        i = (s * 2 + h) * NQ + j
        return rcopy(
            RR.at[s, h, span(j)], RR.at[s + 1, h, span(j)], ring_s + i, ring_r + i,
            {"z": lax.rem(z + NZ + 1 - 2 * h, NZ)},
        )

    def for_core(s, j):
        def step(h, carry):
            ps(s, h, j)[...] = unit(s, h, j, 1 - c).astype(BF16)
            ps_copy(s, h, j).start()
            return carry

        lax.fori_loop(0, 2, step, 0)

    def mine(s, h, j):
        a = unit(s, h, j, c)
        ps_copy(s, h, j).wait_recv()
        return a + ps(s, h, j, D // 2)[...].astype(F32)

    def with_ring(s, h, j):
        a = mine(s, h, j)
        ring_copy(s - 1, h, j).wait_recv()
        return a + RR[s, h, span(j), :].astype(F32)

    def own(s, j, get):
        def step(h, carry):
            RR[s, h, span(j), :] = get(s, h, j).astype(BF16)
            ring_copy(s, h, j).start()
            return carry

        lax.fori_loop(0, 2, step, 0)

    phase("grad0")
    gradient(0)
    phase("core00")
    for_core(0, 0)
    phase("grad1")
    gradient(1)
    send_rows(0)
    phase("own00")
    own(0, 0, mine)
    phase("core01")
    for_core(0, 1)
    phase("grad2")
    gradient(2)
    phase("own01")
    own(0, 1, mine)
    phase("core02")
    for_core(0, 2)
    phase("grad3")
    gradient(3)
    send_rows(1)
    phase("own02")
    own(0, 2, mine)
    phase("core03")
    for_core(0, 3)
    for_core(1, 0)
    phase("own03")
    own(0, 3, mine)
    phase("core1")
    for j in range(1, NQ):
        for_core(1, j)

    phase("losses")
    sums = [jnp.sum(jnp.where(jobs == float(j), loss, 0.0), axis=0, keepdims=True) for j in range(JOBS)]
    JL[y] = jnp.concatenate(sums, axis=0)
    jn = take("r", 3)
    for r in (1, 3, 2):
        send(JL.at[y], JL.at[y], jn + r - 1, {"y": yn(r)})
    for q in range(3):
        n = min(128, T - q * 128)
        t = COL2[pl.ds(al(x * T + q * 128, 8), n), :]
        if n < 128:
            t = jnp.concatenate([t, jnp.zeros((128 - n, 128), F32)], axis=0)
        small[0:1, q * 128 : (q + 1) * 128] = t.T[3:4]
    for r in (1, 3, 2):
        got(JL.at[lax.rem(y + NY - r, NY)], jn + r - 1)
    total = jnp.sum(JL[0] + JL[1] + JL[2] + JL[3], axis=1, keepdims=True) / counts
    total = jnp.concatenate([jnp.broadcast_to(total, (8, 128)), jnp.zeros((120, 128), F32)], axis=0)
    small[0:1, 384:512] = total.T[0:1]

    phase("ring")

    def ring_step(s, carry):
        for j in range(NQ):
            own(s, j, with_ring)
            for_core(s + 1, j)
        return carry

    lax.fori_loop(1, NZ - 1, ring_step, 0)

    xr = take("r", 3 * NQ)
    ag = take("r", 3 * NQ)
    cc = take("r", 4 * 2 * NQ)

    def hg_cols(zz, core, h):
        return pl.ds(al(((NC * core + h) * NY + zz) * DB, DB), DB)

    def spread(src, zz, j, sem):
        for h in range(2):
            piece = src.at[pl.ds(OFF[j], LEN[j]), pl.ds(h * CW, CW)]
            dst = hg.at[pl.ds(OFF[j], LEN[j]), hg_cols(zz, c, h)]
            send(piece, dst, sem + h, other)
            load(piece, dst, outs)

    def last(j):
        part = pl.ds(OFF[j], LEN[j])
        phase("last%d" % j)
        for h in range(2):
            a = with_ring(NZ - 1, h, j)
            XS[:, OFF[j] : OFF[j] + LEN[j], h * CW : (h + 1) * CW] = a.astype(BF16).reshape(NX, LEN[j], CW)
        for r in (2, 1, 3):
            send(XS.at[xn(r), part], XR.at[r - 1, part], xr + j * 3 + r - 1, {"x": xn(r)})

    def x_sum(j):
        part = pl.ds(OFF[j], LEN[j])
        phase("xsum%d" % j)
        total = XS[x, part, :].astype(F32)
        for r in (1, 3, 2):
            got(XR.at[r - 1, part], xr + j * 3 + r - 1)
            total = total + XR[r - 1, part, :].astype(F32)
        FO[part, :] = total.astype(BF16)
        for r in (2, 1, 3):
            send(FO.at[part], AG.at[r - 1, part], ag + j * 3 + r - 1, {"z": zn(r)})
        spread(FO, z, j, cc + j * 8)

    def gather(j):
        part = pl.ds(OFF[j], LEN[j])
        phase("gather%d" % j)
        for r in (1, 3, 2):
            got(AG.at[r - 1, part], ag + j * 3 + r - 1)
            spread(AG.at[r - 1], lax.rem(z + NZ - r, NZ), j, cc + j * 8 + 2 * r)

    last(0)
    last(1)
    x_sum(0)
    last(2)
    x_sum(1)
    last(3)
    x_sum(2)
    gather(0)
    x_sum(3)
    gather(1)
    gather(2)
    gather(3)

    phase("arrivals")
    for k in range(NK):
        for r in ORDER:
            cols = al(xp(r) * U + k * CW, CW)
            got(lg.at[:, pl.ds(cols, CW)], lgs + k * 3 + r - 1)
            lg_remote(k, r).wait_send()
        lg_local(k).wait()
    for i in range(2):
        for r in ORDER:
            part = pl.ds(OFF[2 * i], LEN[2 * i] * 2)
            got(gr.at[part, pl.ds(al(xp(r) * U, U), U)], grs + i * 3 + r - 1)
    for j in range(NQ):
        rows = pl.ds(OFF[j], LEN[j])
        for h in range(2):
            got(hg.at[rows, hg_cols(z, 1 - c, h)], cc + j * 8 + h)
            for r in (1, 3, 2):
                got(hg.at[rows, hg_cols(lax.rem(z + NZ - r, NZ), 1 - c, h)], cc + j * 8 + 2 * r + h)
    for s in range(NZ):
        for h in range(2):
            for j in range(NQ):
                ps_copy(s, h, j).wait_send()
                if s < NZ - 1:
                    ring_copy(s, h, j).wait_send()
    phase("drain")
    drain_sends(pending)
    drain(outs)
    phase(None)
    assert used["s"] <= NSEND and used["r"] <= NRECV and used["l"] <= NLOAD, used


NSEND, NRECV, NLOAD = 320, 304, 112


def vmem(*shape, dtype=BF16):
    return pltpu.VMEM(shape, dtype)


def shards(hidden, weight, down, up, labels, jobs):
    hbm = pl.BlockSpec(memory_space=pl.ANY)
    vm = pl.BlockSpec(memory_space=pltpu.VMEM)
    logits, rows, grad, small = pl.pallas_call(
        kernel,
        out_shape=(
            jax.ShapeDtypeStruct((T, V), BF16),
            jax.ShapeDtypeStruct((T, V), BF16),
            jax.ShapeDtypeStruct((T, D), BF16),
            jax.ShapeDtypeStruct((1, 512), F32),
        ),
        in_specs=[hbm] * 4 + [vm],
        out_specs=(hbm, hbm, hbm, vm),
        scratch_shapes=[
            vmem(S, D),
            vmem(D, U + 256),
            vmem(DB, V),
            vmem(NK, S, CW, dtype=F32),
            vmem(S, U),
            vmem(NX, T, U + 256),
            vmem(NZ, 2, S, CW),
            vmem(NX, T, SH),
            vmem(3, T, SH),
            vmem(T, SH),
            vmem(3, T, SH),
            vmem(S, 128, dtype=F32),
            vmem(S, 128, dtype=F32),
            vmem(S, 128),
            vmem(128, U),
            vmem(NX, 3, 8, 128, dtype=F32),
            vmem(NZ * NC, 3, 16, 128, dtype=F32),
            vmem(NX, 3, 16, 128, dtype=F32),
            vmem(16, 128, dtype=F32),
            vmem(NY, 8, 128, dtype=F32),
            vmem(NY, 8, 128, dtype=F32),
            pltpu.SemaphoreType.DMA((NSEND,)),
            pltpu.SemaphoreType.DMA((NRECV,)),
            pltpu.SemaphoreType.DMA((NLOAD,)),
        ],
        compiler_params=pltpu.CompilerParams(
            collective_id=0, has_side_effects=True, vmem_limit_bytes=58 * 1024 * 1024
        ),
        name="step",
    )(hidden, weight, down, up, jnp.stack([labels, jobs]))
    return logits, rows, grad, small[0, :T], small[0, 384 : 384 + JOBS]


def solution(mesh):
    split = Mesh(mesh.devices.reshape(NZ, NC, NX, NY), ("z", "c", "x", "y"))
    dp, vocab = ("x", "y"), ("z", "c")
    return jax.shard_map(
        shards,
        mesh=split,
        in_specs=(P(dp, None), P(dp, vocab), P(), P(None, vocab), P(dp), P(dp)),
        out_specs=(P(dp, vocab), P(dp, vocab), P(dp, None), P(dp), P()),
        check_vma=False,
    )
```

time: 206 us -> 188 us (0.913)
  Pallas kernels: 191 us -> 174 us
    pallas_call x1, Pallas kernels: 191 us -> 174 us  [shards(): pl.pallas_call(kernel, out_shape=(jax.ShapeDtypeStruct((T, V), BF16), jax...]
where the time goes in v3:
time: 188 us; the launch traced here: 187 us
  Pallas kernels  174 us (93%)
  local copies, waits for them, and re-layouts  12.1 us (6%)
    pallas_call x1, Pallas kernels, shards(): pl.pallas_call(kernel, out_shape=(jax.ShapeDtypeStruct((T, V), BF16), jax...  174 us
    unnamed x7, local copies, waits for them, and re-layouts  8.3 us

profile of v3, /device:TPU:1, one launch (start us, length us, event | category | flops | bytes accessed | tf_op | source)
XLA Modules:
  0.0 187.5 jit_solution(2143254021392352926)
XLA Ops:
  0.6 0.7 stack.10
  1.3 0.7 stack.9
  2.0 0.6 pad_add_fusion.ids_in
  2.6 174.2 %step.1 = (bf16[352,4096]{1,0:T(8,128)(2,1)}, bf16[352,4096]{1,0:T(8,128)(2,1)}, bf16[352,4096]{1,0:T(8,128)(2,1)}, f32[1,512]{1,0:T(1,128)}) custom-call(bf16[352,4096]{1,0:T(8,128)(2,1)} %hid.1, bf16[256,4096]{1,0:T(8,128)(2,1)} %w.1, bf16[4096,128]{1,0:T(8,128)(2,1)} %ad.1, bf16[128,4096]{1,0:T(8,128)(2,1)} %au.1, s32[2,352]{1,0:T(2,128)} %pad_add_fusion.ids_in), custom_call_target="tpu_custom_call" | custom-call | tf_op jit(solution)/shard_map/step/pallas_call | solution.py:706
  176.8 1.2 slice_reduce_fusion
  178.0 1.2 slice_bitcast_fusion
  179.2 0.0 copy-start.1
  179.2 3.9 %copy.14 = bf16[352,4096]{1,0:T(8,128)(2,1)} copy(bf16[352,4096]{1,0:T(8,128)(2,1)} %get-tuple-element.18) | data formatting | bytes 5767168
  183.1 0.0 copy-done.1
  183.1 0.0 copy-start
  183.1 1.6 copy.15
  184.6 1.3 copy-done
  185.9 1.6 copy.16
Async XLA Ops:
  179.2 3.9 %copy-start.1 = (bf16[352,4096]{1,0:T(8,128)(2,1)S(1)}, bf16[352,4096]{1,0:T(8,128)(2,1)}, u32[]{:S(2)}) copy-start(bf16[352,4096]{1,0:T(8,128)(2,1)} %get-tuple-element.19) | copy-start | bytes 8650756
  183.1 2.9 %copy-start = (bf16[352,4096]{1,0:T(8,128)(2,1)S(1)}, bf16[352,4096]{1,0:T(8,128)(2,1)}, u32[]{:S(2)}) copy-start(bf16[352,4096]{1,0:T(8,128)(2,1)} %get-tuple-element.20) | copy-start | bytes 8650756

commit v4 on v3

v4 whole, which is shorter than its diff:
```python
import functools

import jax
import jax.numpy as jnp
from jax import lax
from jax.experimental import pallas as pl
from jax.experimental.pallas import tpu as pltpu
from jax.sharding import Mesh
from jax.sharding import PartitionSpec as P

MESH = pl.DeviceIdType.MESH
F32 = jnp.float32
BF16 = jnp.bfloat16

JOBS = 8
RANK = 16
NX = NY = NZ = 4
NC = 2
T = 352
S = NX * T
HT = T // 2
LEN = (96, 96, 80, 80)
OFF = (0, 96, 192, 272)
NQ = len(LEN)
D = 4096
DB = D // (NX * NY)
V = 4096
U = V // NX
CW = 256
NK = U // CW
SH = D // (NZ * NC)
TOKENS = S * NY
NB = S // 128


def fdot(a, b):
    return jnp.dot(a, b, preferred_element_type=F32)


def tdot(a, b):
    return lax.dot_general(a, b, (((1,), (1,)), ((), ())), preferred_element_type=F32)


def kernel(
    hid, w, ad, au, lab_in, job_in,
    lg, gr, hg, small,
    H, W5, WS, E, LT, G5, RR, XS, XR, FO, COL, COL2, LI, AU, AX, STA, STB, JR, CN, JL,
    ssem, rsem, lsem,
):
    z, c, x, y = (lax.axis_index(a) for a in ("z", "c", "x", "y"))
    v = z * NC + c

    def al(i, m):
        return pl.multiple_of(i, m)

    def xn(r):
        return lax.rem(x + r, NX)

    def yn(r):
        return lax.rem(y + r, NY)

    def zn(r):
        return lax.rem(z + r, NZ)

    used = {"s": 0, "r": 0, "l": 0}

    def take(kind, n=1):
        at = used[kind]
        used[kind] = at + n
        return at

    def rcopy(src, dst, si, ri, dev):
        return pltpu.make_async_remote_copy(
            src_ref=src, dst_ref=dst, send_sem=ssem.at[si], recv_sem=rsem.at[ri],
            device_id=dev, device_id_type=MESH,
        )

    def send(src, dst, si, ri, dev):
        rcopy(src, dst, si, ri, dev).start()

    def got(ref, ri):
        rcopy(ref, ref, 0, ri, {"x": xn(1)}).wait_recv()

    def sent(ref, si):
        rcopy(ref, ref, si, 0, {"x": xn(1)}).wait_send()

    def load(src, dst, li):
        pltpu.make_async_copy(src, dst, lsem.at[li]).start()

    def loaded(ref, li):
        pltpu.make_async_copy(ref, ref, lsem.at[li]).wait()

    scope = []

    def phase(name):
        if scope:
            scope.pop().__exit__(None, None, None)
        if name:
            scope.append(jax.named_scope(name))
            scope[0].__enter__()

    phase("entry")
    bar = pltpu.get_barrier_semaphore()
    peers = (
        [{"x": xn(r)} for r in (1, 2, 3)]
        + [{"y": yn(r)} for r in (1, 2, 3)]
        + [{"z": zn(a), "c": lax.rem(c + b, NC)} for a in range(NZ) for b in range(NC) if a or b]
    )
    for dev in peers:
        pl.semaphore_signal(bar, inc=1, device_id=dev, device_id_type=MESH)

    l_w, l_own, l_h, l_up, l_down = (take("l") for _ in range(5))
    load(w, WS, l_w)
    own_rows = pl.ds(al((y * NX + x) * DB, DB), DB)
    load(w.at[:, pl.ds(al(x * U, U), U)], W5.at[own_rows, pl.ds(0, U)], l_own)
    for p in range(NX * NY):
        n = (p % NX) * NY + p // NX
        load(hid.at[:, pl.ds(n * DB, DB)], H.at[pl.ds(al(x * T, 16), T), pl.ds(p * DB, DB)], l_h)
    load(au.at[:, pl.ds(al(x * U, U), U)], AU, l_up)
    for p in range(NX * NY):
        n = (p % NX) * NY + p // NX
        for q in range(2):
            load(
                ad.at[pl.ds(n * DB, DB), :],
                W5.at[pl.ds(p * DB, DB), pl.ds(U + q * 128, 128)],
                l_down,
            )
    for q in range(3):
        n = min(128, T - q * 128)
        AX[x, q] = jnp.full((8, 128), -1.0, F32)
        AX[x, q, 0:1, 0:n] = lab_in[pl.ds(q * 128, n)].astype(F32).reshape(1, n)
        AX[x, q, 1:2, 0:n] = job_in[pl.ds(q * 128, n)].astype(F32).reshape(1, n)
    pl.semaphore_wait(bar, len(peers))

    ORDER = (1, 3, 2)
    wx = take("r", NK * 3)
    hx = take("r", 3)
    ax, lgs, cn, sa, sb, grs, jn, cc = (take("r") for _ in range(8))
    wy = take("r", NK * 5)
    hz = take("r", 3 * 3)
    hc = take("r", 3)
    ws_s, h_s, ax_s, lg_s, cn_s, sa_s, sb_s, gr_s, cs_s, ring_s, jn_s, x_s, ag_s, cc_s = (
        take("s") for _ in range(14)
    )

    def xp(r):
        return lax.rem(x + NX - r, NX)

    def wblock(row, k):
        return W5.at[row, pl.ds(k * CW, CW)]

    def send_w(k):
        for r in ORDER:
            send(
                WS.at[:, pl.ds(al(xn(r) * U + k * CW, CW), CW)],
                wblock(own_rows, k), ws_s, wx + k * 3 + r - 1, {"x": xn(r)},
            )

    def piece(dy, r, k):
        return wblock(pl.ds(al((yn(dy) * NX + xp(r)) * DB, DB), DB), k)

    def y_own(k, r):
        src = piece(0, r, k)
        if r:
            got(src, wx + k * 3 + r - 1)
        at = wy + k * 5
        send(src, src, ws_s, at + (r if r in (0, 2) else 4), {"y": yn(1)})
        send(src, src, ws_s, at + (4 if r in (0, 2) else r), {"y": yn(3)})

    def y_fwd(k, r):
        at = wy + k * 5
        src = piece(3 if r in (0, 2) else 1, r, k)
        got(src, at + r)
        send(src, src, ws_s, at + 4, {"y": yn(1 if r in (0, 2) else 3)})

    def w_end(k):
        got(wblock(pl.ds(0, 8 * DB), k), wy + k * 5 + 4)

    other = {"c": 1 - c}

    def hpiece(xb, share, lo=0, n=T):
        return H.at[pl.ds(al(xb * T + lo, 16), n), pl.ds(al(share * SH, SH), SH)]

    def h_send(at, ri, dev):
        send(at, at, h_s, ri, dev)

    def h_in(r):
        mine = hpiece(xp(r), v)
        got(mine, hx + r - 1)
        b = hz + (r - 1) * 3
        h_send(mine, b + 0, {"z": zn(1)})
        h_send(mine, b + 1, {"z": zn(3)})
        h_send(mine, hc + r - 1, other)

    def h_fwd(r):
        xb = xp(r)
        b, d = hz + (r - 1) * 3, hc + r - 1
        left, right = zn(3) * NC + c, zn(1) * NC + c
        got(hpiece(xb, left), b + 0)
        h_send(hpiece(xb, left, 0, HT), b + 2, {"z": zn(1)})
        h_send(hpiece(xb, left), d, other)
        got(hpiece(xb, right), b + 1)
        h_send(hpiece(xb, right, HT, HT), b + 2, {"z": zn(3)})
        h_send(hpiece(xb, right), d, other)

    def h_last(r):
        far = hpiece(xp(r), zn(2) * NC + c)
        got(far, hz + (r - 1) * 3 + 2)
        h_send(far, hc + r - 1, other)

    def h_end(r):
        got(H.at[pl.ds(0, T), pl.ds(0, NZ * SH)], hc + r - 1)

    lane128 = lax.broadcasted_iota(jnp.int32, (T, 128), 1)
    rank_job = (lane128 // RANK).astype(F32)
    base = v * V + x * U
    lane_cw = lax.broadcasted_iota(jnp.int32, (T, CW), 1)
    my_cols = al(x * U, U)

    def lora_in(r):
        rows = pl.ds(al(xp(r) * T, 16), T)
        hit = COL[rows, 1:2] == rank_job
        a = fdot(H[rows, :], W5[:, U : U + 128])
        LI[rows, :] = jnp.where(hit, a, 0.0).astype(BF16)

    def lg_cols(k):
        return pl.ds(al(my_cols + k * CW, CW), CW)

    def lg_remote(k, r):
        src = LT.at[pl.ds(al(xp(r) * T, 16), T), pl.ds(al(k * CW, CW), CW)]
        send(src, lg.at[:, lg_cols(k)], lg_s, lgs, {"x": xp(r)})

    def lg_local(k):
        cols = pl.ds(al(k * CW, CW), CW)
        lg[:, lg_cols(k)] = LT[pl.ds(al(x * T, 16), T), cols]

    def task(k, r):
        rows = pl.ds(al(xp(r) * T, 16), T)
        cols = pl.ds(al(k * CW, CW), CW)
        a = fdot(H[rows, :], W5[:, cols])
        a = a + fdot(LI[rows, :], AU[:, cols])
        LT[rows, cols] = a.astype(BF16)
        top = jnp.max(a, axis=1, keepdims=True)
        e = jnp.exp(a - top)
        E[k, rows, :] = e
        total = jnp.sum(e, axis=1, keepdims=True)
        ids = (lane_cw + (base + k * CW)).astype(F32)
        target = jnp.sum(jnp.where(ids == COL[rows, 0:1], a, 0.0), axis=1, keepdims=True)
        old = COL[rows, :]
        old = jnp.where(lane128 == 8 + k, top, old)
        old = jnp.where(lane128 == 12 + k, total, old)
        COL[rows, :] = jnp.where(lane128 == 16 + k, target, old)

    def tasks(k0, nk, o0, no, out=True):
        def step(i, carry):
            k, o = k0 + i // no, o0 + lax.rem(i, no)
            r = jnp.where(o == 2, 3, jnp.where(o == 3, 2, o))
            task(k, r)
            if not out:
                return carry
            if o0:
                lg_remote(k, r)
            else:
                pl.when(r > 0)(lambda: lg_remote(k, r))
                pl.when(r == 0)(lambda: lg_local(k))
            return carry

        lax.fori_loop(0, nk * no, step, 0)

    loaded(WS, l_w)
    loaded(W5.at[own_rows, pl.ds(0, U)], l_own)
    send_w(0)
    for r in ORDER:
        send(AX.at[x], AX.at[x], ax_s, ax, {"x": xn(r)})
    for k in range(3):
        y_own(k, 0)
    loaded(H.at[pl.ds(0, T), :], l_h)

    def send_h(r):
        send(hpiece(x, v), hpiece(x, v), h_s, hx + r - 1, {"x": xn(r)})

    send_h(1)
    send_h(3)
    send_w(1)
    send_h(2)
    send_w(2)
    send_w(3)
    phase("p1a")
    y_fwd(0, 0)
    for r in ORDER:
        y_own(0, r)
    y_own(3, 0)
    phase("h_in13")
    h_in(1)
    h_in(3)
    y_fwd(1, 0)
    phase("p1c")
    y_fwd(0, 1)
    y_fwd(0, 3)
    phase("p1b")
    for r in ORDER:
        y_own(1, r)
    y_fwd(0, 2)
    phase("cols")

    got(AX.at[0:3], ax)
    sub = lax.broadcasted_iota(jnp.int32, (8, 128), 0).astype(F32)
    counts = jnp.zeros((8, 128), F32)
    for xb in range(NX):
        for q in range(3):
            tile = AX[xb, q]
            n = min(128, T - q * 128)
            turned = jnp.concatenate([tile, jnp.zeros((120, 128), F32)], axis=0).T
            COL[pl.ds(xb * T + q * 128, n), :] = turned[:n]
            counts = counts + (tile[1:2, :] == sub).astype(F32)
    CN[y] = counts
    for r in (1, 3, 2):
        send(CN.at[y], CN.at[y], cn_s, cn, {"y": yn(r)})
    loaded(AU, l_up)
    loaded(W5.at[:, pl.ds(U, 256)], l_down)
    lora_in(0)
    phase("h_fwd1")
    h_fwd(1)
    phase("p1e")
    y_fwd(1, 1)
    y_fwd(1, 3)
    phase("h_in2")
    h_in(2)
    phase("p1f")
    y_fwd(1, 2)
    phase("w_end0")
    w_end(0)
    phase("t0_0")
    tasks(0, 1, 0, 1)
    phase("y_own2")
    for r in ORDER:
        y_own(2, r)
    phase("h_fwd3")
    h_fwd(3)
    phase("y_own3")
    for r in ORDER:
        y_own(3, r)
    phase("w_end1")
    w_end(1)
    phase("t1_0")
    tasks(1, 1, 0, 1)
    phase("h_last1")
    h_last(1)
    h_end(1)
    phase("t01_1")
    lora_in(1)
    tasks(0, 2, 1, 1)
    phase("y_fwd2")
    for r in (0, 1, 3, 2):
        y_fwd(2, r)
    phase("h_fwd2")
    h_fwd(2)
    phase("h_last3")
    h_last(3)
    phase("y_fwd3")
    y_fwd(3, 0)
    y_fwd(3, 1)
    phase("h_end3")
    h_end(3)
    phase("t01_3")
    lora_in(3)
    tasks(0, 2, 2, 1)
    phase("y_fwd3b")
    y_fwd(3, 3)
    y_fwd(3, 2)
    phase("h_last2")
    h_last(2)
    h_end(2)
    phase("t01_2")
    lora_in(2)
    tasks(0, 2, 3, 1)
    sent(H.at[pl.ds(0, 3 * T), :], h_s)
    phase("w_end2")
    w_end(2)
    phase("t2")
    tasks(2, 1, 0, 4)
    phase("w_end3")
    w_end(3)
    phase("t3")
    tasks(3, 1, 0, 4, False)
    phase("stats_a")

    STA[v] = jnp.broadcast_to(jnp.ones((1, 1, 1), F32), (3, 16, 128))
    JR[...] = jnp.full((16, 128), -1.0, F32)
    for b in range(NB):
        t = COL[b * 128 : (b + 1) * 128, :].T
        m, e, g = t[8:12], t[12:16], t[16:20]
        top = jnp.max(m, axis=0, keepdims=True)
        STA[v, 0, b : b + 1, :] = top
        STA[v, 1, b : b + 1, :] = jnp.sum(e * jnp.exp(m - top), axis=0, keepdims=True)
        STA[v, 2, b : b + 1, :] = jnp.sum(g, axis=0, keepdims=True)
        JR[b : b + 1, :] = t[1:2]
    turns = [(a, b) for a in (2, 1, 3, 0) for b in range(NC) if a or b]
    for a, b in turns:
        dev = {"z": zn(a), "c": lax.rem(c + b, NC)}
        send(STA.at[v], STA.at[v], sa_s, sa, dev)
    phase("counts")
    got(CN.at[0:3], cn)
    counts = jnp.sum(CN[0] + CN[1] + CN[2] + CN[3], axis=1, keepdims=True)
    counts = jnp.maximum(counts, 1.0)
    per_job = TOKENS / (JOBS * counts)
    jobs = JR[...]
    weight = jnp.zeros((16, 128), F32)
    for j in range(JOBS):
        weight = jnp.where(jobs == float(j), per_job[j : j + 1, :], weight)
    phase("stats_w")
    got(STA.at[0:7], sa)

    def joined(ref, n):
        top = functools.reduce(jnp.maximum, [ref[i, 0] for i in range(n)])
        e = functools.reduce(jnp.add, [ref[i, 1] * jnp.exp(ref[i, 0] - top) for i in range(n)])
        return top, e, functools.reduce(jnp.add, [ref[i, 2] for i in range(n)])

    STB[x, 0], STB[x, 1], STB[x, 2] = joined(STA, NZ * NC)
    phase("stats_b")
    for r in (2, 1, 3):
        send(STB.at[x], STB.at[x], sb_s, sb, {"x": xn(r)})
    for r in ORDER:
        lg_remote(NK - 1, r)
    lg_local(NK - 1)
    got(STB.at[0:3], sb)
    phase("finish")
    top, e, g = joined(STB, NX)
    loss = top + jnp.log(e) - g
    scaled = weight / e
    blank = jnp.zeros((124, 128), F32)
    for b in range(NB):
        parts = [i[b : b + 1] for i in (top, scaled, weight, loss)]
        COL2[b * 128 : (b + 1) * 128, :] = jnp.concatenate(parts + [blank], axis=0).T

    def gradient(j):
        part = pl.ds(OFF[j], LEN[j])

        def step(m, carry):
            rows = pl.ds(al(m * T + OFF[j], 16), LEN[j])
            lab = COL[rows, 0:1]
            weight = COL2[rows, 2:3]
            for k in range(NK):
                f = jnp.exp(COL[rows, 8 + k : 9 + k] - COL2[rows, 0:1]) * COL2[rows, 1:2]
                ids = (lane_cw[: LEN[j]] + (base + k * CW)).astype(F32)
                g = E[k, rows, :] * f - jnp.where(ids == lab, weight, 0.0)
                G5[m, part, k * CW : (k + 1) * CW] = g.astype(BF16)
            return carry

        lax.fori_loop(0, NX, step, 0)
        rows = G5[:, OFF[j] : OFF[j] + LEN[j], 0:U].reshape(NX * LEN[j], U)
        lora = tdot(rows, AU[...]).reshape(NX, LEN[j], 128)
        for m in range(NX):
            job = COL[m * T + OFF[j] : m * T + OFF[j] + LEN[j], 1:2]
            one = jnp.where(job == rank_job[: LEN[j]], lora[m], 0.0)
            high = one.astype(BF16)
            G5[m, part, U : U + 128] = high
            G5[m, part, U + 128 : U + 256] = (one - high.astype(F32)).astype(BF16)

    def send_rows(i):
        part = pl.ds(OFF[2 * i], LEN[2 * i] * 2)
        for r in ORDER:
            send(G5.at[xn(r), part, pl.ds(0, U)], gr.at[part, pl.ds(my_cols, U)], gr_s, grs, {"x": xn(r)})
        gr[part, pl.ds(my_cols, U)] = G5[x, part, 0:U]

    cs_r = take("r", 32)
    ring_r = take("r", 24)

    def zt(s, h):
        return lax.rem(z + NZ + (2 * h - 1) * (s + 1), NZ)

    def span(j):
        return pl.ds(NX * OFF[j], NX * LEN[j])

    def unit(s, h, j, core):
        at = al((zt(s, h) * NC + core) * SH + h * CW, CW)
        g = G5[:, OFF[j] : OFF[j] + LEN[j], :].reshape(NX * LEN[j], U + 256)
        return tdot(g, W5[pl.ds(at, CW), :])

    def ps(s, h, j, at=0):
        return H.at[span(j), pl.ds(al(at + (s * 2 + h) * CW, CW), CW)]

    def ps_copy(s, h, j):
        i = (s * 2 + h) * NQ + j
        return rcopy(ps(s, h, j), ps(s, h, j, D // 2), cs_s, cs_r + i, other)

    def ring_copy(s, h, j):
        i = (s * 2 + h) * NQ + j
        return rcopy(
            RR.at[s, h, span(j)], RR.at[s + 1, h, span(j)], ring_s, ring_r + i,
            {"z": lax.rem(z + NZ + 1 - 2 * h, NZ)},
        )

    def for_core(s, j):
        def step(h, carry):
            ps(s, h, j)[...] = unit(s, h, j, 1 - c).astype(BF16)
            ps_copy(s, h, j).start()
            return carry

        lax.fori_loop(0, 2, step, 0)

    def mine(s, h, j):
        a = unit(s, h, j, c)
        ps_copy(s, h, j).wait_recv()
        return a + ps(s, h, j, D // 2)[...].astype(F32)

    def with_ring(s, h, j):
        a = mine(s, h, j)
        ring_copy(s - 1, h, j).wait_recv()
        return a + RR[s, h, span(j), :].astype(F32)

    def own(s, j, get):
        def step(h, carry):
            RR[s, h, span(j), :] = get(s, h, j).astype(BF16)
            ring_copy(s, h, j).start()
            return carry

        lax.fori_loop(0, 2, step, 0)

    phase("grad0")
    gradient(0)
    phase("core00")
    for_core(0, 0)
    phase("own00")
    own(0, 0, mine)
    phase("grad1")
    gradient(1)
    send_rows(0)
    phase("core01")
    for_core(0, 1)
    phase("grad2")
    gradient(2)
    phase("own01")
    own(0, 1, mine)
    phase("core02")
    for_core(0, 2)
    phase("grad3")
    gradient(3)
    send_rows(1)
    phase("own02")
    own(0, 2, mine)
    phase("core03")
    for_core(0, 3)
    for_core(1, 0)
    phase("own03")
    own(0, 3, mine)
    phase("core1")
    for j in range(1, NQ):
        for_core(1, j)

    phase("losses")
    sums = [jnp.sum(jnp.where(jobs == float(j), loss, 0.0), axis=0, keepdims=True) for j in range(JOBS)]
    JL[y] = jnp.concatenate(sums, axis=0)
    for r in (1, 3, 2):
        send(JL.at[y], JL.at[y], jn_s, jn, {"y": yn(r)})
    for q in range(3):
        n = min(128, T - q * 128)
        t = COL2[pl.ds(al(x * T + q * 128, 8), n), :]
        if n < 128:
            t = jnp.concatenate([t, jnp.zeros((128 - n, 128), F32)], axis=0)
        small[0:1, q * 128 : (q + 1) * 128] = t.T[3:4]
    got(JL.at[0:3], jn)
    total = jnp.sum(JL[0] + JL[1] + JL[2] + JL[3], axis=1, keepdims=True) / counts
    total = jnp.concatenate([jnp.broadcast_to(total, (8, 128)), jnp.zeros((120, 128), F32)], axis=0)
    small[0:1, 384:512] = total.T[0:1]

    phase("ring")

    def ring_step(s, carry):
        for j in range(NQ):
            own(s, j, with_ring)
            for_core(s + 1, j)
        return carry

    lax.fori_loop(1, NZ - 1, ring_step, 0)

    xr = take("r", NQ)
    ag = take("r", 3 * NQ)

    def hg_at(zz, j, h):
        cols = pl.ds(al(((NC * c + h) * NY + zz) * DB, DB), DB)
        return hg.at[pl.ds(OFF[j], LEN[j]), cols]

    def last(j):
        part = pl.ds(OFF[j], LEN[j])
        phase("last%d" % j)
        for h in range(2):
            a = with_ring(NZ - 1, h, j)
            XS[:, OFF[j] : OFF[j] + LEN[j], h * CW : (h + 1) * CW] = a.astype(BF16).reshape(NX, LEN[j], CW)
        for r in (2, 1, 3):
            send(XS.at[xn(r), part], XR.at[r - 1, part], x_s, xr + j, {"x": xn(r)})

    def x_sum(j):
        part = pl.ds(OFF[j], LEN[j])
        phase("xsum%d" % j)
        got(XR.at[:, part], xr + j)
        total = XS[x, part, :].astype(F32)
        for r in (1, 3, 2):
            total = total + XR[r - 1, part, :].astype(F32)
        FO[part, :] = total.astype(BF16)
        for h in range(2):
            src = FO.at[part, pl.ds(h * CW, CW)]
            for r in (2, 1, 3):
                send(src, hg_at(z, j, h), ag_s, ag + j * 3 + r - 1, {"z": zn(r)})
            send(src, hg_at(z, j, h), cc_s, cc, other)
            hg_at(z, j, h)[...] = FO[part, h * CW : (h + 1) * CW]

    def gather(j):
        phase("gather%d" % j)
        for r in (1, 3, 2):
            got(hg.at[pl.ds(OFF[j], LEN[j]), pl.ds(0, SH)], ag + j * 3 + r - 1)
            for h in range(2):
                src = hg_at(lax.rem(z + NZ - r, NZ), j, h)
                send(src, src, cc_s, cc, other)

    last(0)
    last(1)
    x_sum(0)
    last(2)
    x_sum(1)
    last(3)
    x_sum(2)
    gather(0)
    x_sum(3)
    gather(1)
    gather(2)
    gather(3)

    phase("arrivals")
    got(lg.at[:, pl.ds(0, 3 * U)], lgs)
    got(gr.at[:, pl.ds(0, 3 * U)], grs)
    got(hg.at[:, pl.ds(0, NZ * SH)], cc)
    phase("drain")
    sent(W5.at[pl.ds(0, 60 * DB // NX), pl.ds(0, U)], ws_s)
    sent(AX.at[0:3], ax_s)
    sent(lg.at[:, pl.ds(0, 3 * U)], lg_s)
    sent(CN.at[0:3], cn_s)
    sent(STA.at[0:7], sa_s)
    sent(STB.at[0:3], sb_s)
    sent(gr.at[:, pl.ds(0, 3 * U)], gr_s)
    sent(H.at[:, pl.ds(0, D // 2)], cs_s)
    sent(RR.at[0:3], ring_s)
    sent(JL.at[0:3], jn_s)
    sent(XR, x_s)
    sent(XR, ag_s)
    sent(hg.at[:, pl.ds(0, NZ * SH)], cc_s)
    phase(None)
    assert used == {"s": NSEND, "r": NRECV, "l": NLOAD}, used


NSEND, NRECV, NLOAD = 14, 127, 5


def emit(lgv, grv, hgv, small, lg, gr, hg, tl, jl, sem):
    copies = [
        pltpu.make_async_copy(src, dst, sem.at[i])
        for i, (src, dst) in enumerate(((lgv, lg), (grv, gr), (hgv, hg)))
    ]
    for d in copies:
        d.start()
    tl[...] = small[0, :T]
    jl[...] = small[0, 384 : 384 + JOBS]
    for d in copies:
        d.wait()


def vmem(*shape, dtype=BF16):
    return pltpu.VMEM(shape, dtype)


def shards(hidden, weight, down, up, labels, jobs):
    hbm = pl.BlockSpec(memory_space=pl.ANY)
    vm = pl.BlockSpec(memory_space=pltpu.VMEM)
    held = pl.pallas_call(
        kernel,
        out_shape=(vmem(T, V), vmem(T, V), vmem(T, D), vmem(1, 512, dtype=F32)),
        in_specs=[hbm] * 4 + [vm] * 2,
        out_specs=(vm, vm, vm, vm),
        scratch_shapes=[
            vmem(S, D),
            vmem(D, U + 256),
            vmem(DB, V),
            vmem(NK, S, CW, dtype=F32),
            vmem(S, U),
            vmem(NX, T, U + 256),
            vmem(NZ, 2, S, CW),
            vmem(NX, T, SH),
            vmem(3, T, SH),
            vmem(T, SH),
            vmem(S, 128, dtype=F32),
            vmem(S, 128, dtype=F32),
            vmem(S, 128),
            vmem(128, U),
            vmem(NX, 3, 8, 128, dtype=F32),
            vmem(NZ * NC, 3, 16, 128, dtype=F32),
            vmem(NX, 3, 16, 128, dtype=F32),
            vmem(16, 128, dtype=F32),
            vmem(NY, 8, 128, dtype=F32),
            vmem(NY, 8, 128, dtype=F32),
            pltpu.SemaphoreType.DMA((NSEND,)),
            pltpu.SemaphoreType.DMA((NRECV,)),
            pltpu.SemaphoreType.DMA((NLOAD,)),
        ],
        compiler_params=pltpu.CompilerParams(
            collective_id=0, has_side_effects=True, vmem_limit_bytes=52 * 1024 * 1024
        ),
        name="step",
    )(hidden, weight, down, up, labels, jobs)
    return pl.pallas_call(
        emit,
        out_shape=(
            jax.ShapeDtypeStruct((T, V), BF16),
            jax.ShapeDtypeStruct((T, V), BF16),
            jax.ShapeDtypeStruct((T, D), BF16),
            jax.ShapeDtypeStruct((T,), F32),
            jax.ShapeDtypeStruct((JOBS,), F32),
        ),
        in_specs=[vm] * 4,
        out_specs=(hbm, hbm, hbm, vm, vm),
        scratch_shapes=[pltpu.SemaphoreType.DMA((3,))],
        compiler_params=pltpu.CompilerParams(vmem_limit_bytes=1024 * 1024),
        name="emit",
    )(*(pltpu.with_memory_space_constraint(i, pltpu.VMEM) for i in held))


def solution(mesh):
    split = Mesh(mesh.devices.reshape(NZ, NC, NX, NY), ("z", "c", "x", "y"))
    dp, vocab = ("x", "y"), ("z", "c")
    return jax.shard_map(
        shards,
        mesh=split,
        in_specs=(P(dp, None), P(dp, vocab), P(), P(None, vocab), P(dp), P(dp)),
        out_specs=(P(dp, vocab), P(dp, vocab), P(dp, None), P(dp), P()),
        check_vma=False,
    )
```

time: 188 us -> 174 us (0.926)
  local copies, waits for them, and re-layouts: 12.1 us -> 0 us
    unnamed x7 -> x0, local copies, waits for them, and re-layouts: 8.3 us -> none
    pallas_call x1 -> x2, Pallas kernels: 174 us -> 173 us  [the longest x1 169 us: shards(): pl.pallas_call(kernel, out_shape=(vmem(T, V), vmem(T, V), vmem(T, D), vme...]
where the time goes in v4:
time: 174 us
  Pallas kernels  173 us (99%)
    pallas_call x1, Pallas kernels, shards(): pl.pallas_call(kernel, out_shape=(vmem(T, V), vmem(T, V), vmem(T, D), vme...  169 us
    pallas_call x1, Pallas kernels, shards(): pl.pallas_call(emit, out_shape=(jax.ShapeDtypeStruct((T, V), BF16), jax.S...  4.07 us

profile of v4, /device:TPU:1, one launch (start us, length us, event | category | flops | bytes accessed | tf_op | source)
XLA Modules:
  0.0 173.8 jit_solution(14851474696842965875)
XLA Ops:
  0.6 168.9 %step.1 = (bf16[352,4096]{1,0:T(8,128)(2,1)S(1)}, bf16[352,4096]{1,0:T(8,128)(2,1)S(1)}, bf16[352,4096]{1,0:T(8,128)(2,1)S(1)}, f32[1,512]{1,0:T(1,128)S(1)}) custom-call(bf16[352,4096]{1,0:T(8,128)(2,1)} %hid.1, bf16[256,4096]{1,0:T(8,128)(2,1)} %w.1, bf16[4096,128]{1,0:T(8,128)(2,1)} %ad.1, bf16[128,4096]{1,0:T(8,128)(2,1)} %au.1, s32[352]{0:T(512)} %lab_in.1, ...), custom_call_target="tpu_custom_call" | custom-call | tf_op jit(solution)/shard_map/step/pallas_call | solution.py:674
  169.5 4.1 %emit.1 = (bf16[352,4096]{1,0:T(8,128)(2,1)}, bf16[352,4096]{1,0:T(8,128)(2,1)}, bf16[352,4096]{1,0:T(8,128)(2,1)}, f32[352]{0:T(512)}, f32[8]{0:T(128)}) custom-call(bf16[352,4096]{1,0:T(8,128)(2,1)S(1)} %get-tuple-element.9.lgv, bf16[352,4096]{1,0:T(8,128)(2,1)S(1)} %get-tuple-element.10.grv, bf16[352,4096]{1,0:T(8,128)(2,1)S(1)} %get-tuple-element.11.hgv, ...), custom_call_target="tpu_custom_call" | custom-call | tf_op jit(solution)/shard_map/emit/pallas_call | solution.py:709

commit v5 on v4

--- a/solution.py
+++ b/solution.py
@@ -19,8 +19,8 @@
 T = 352
 S = NX * T
 HT = T // 2
-LEN = (96, 96, 80, 80)
-OFF = (0, 96, 192, 272)
+LEN = (80, 112, 96, 64)
+OFF = (0, 80, 192, 288)
 NQ = len(LEN)
 D = 4096
 DB = D // (NX * NY)
@@ -136,7 +136,7 @@
     wx = take("r", NK * 3)
     hx = take("r", 3)
     ax, lgs, cn, sa, sb, grs, jn, cc = (take("r") for _ in range(8))
-    wy = take("r", NK * 5)
+    wy = take("r", NK * 6)
     hz = take("r", 3 * 3)
     hc = take("r", 3)
     ws_s, h_s, ax_s, lg_s, cn_s, sa_s, sb_s, gr_s, cs_s, ring_s, jn_s, x_s, ag_s, cc_s = (
@@ -163,18 +163,25 @@
         src = piece(0, r, k)
         if r:
             got(src, wx + k * 3 + r - 1)
-        at = wy + k * 5
+        at = wy + k * 6
         send(src, src, ws_s, at + (r if r in (0, 2) else 4), {"y": yn(1)})
         send(src, src, ws_s, at + (4 if r in (0, 2) else r), {"y": yn(3)})
 
     def y_fwd(k, r):
-        at = wy + k * 5
+        at = wy + k * 6
         src = piece(3 if r in (0, 2) else 1, r, k)
         got(src, at + r)
-        send(src, src, ws_s, at + 4, {"y": yn(1 if r in (0, 2) else 3)})
+        send(src, src, ws_s, at + 5, {"y": yn(1 if r in (0, 2) else 3)})
+
+    def w_near(k):
+        got(wblock(pl.ds(0, 4 * DB), k), wy + k * 6 + 4)
+
+    def w_far(k):
+        got(wblock(pl.ds(0, 4 * DB), k), wy + k * 6 + 5)
 
     def w_end(k):
-        got(wblock(pl.ds(0, 8 * DB), k), wy + k * 5 + 4)
+        w_near(k)
+        w_far(k)
 
     other = {"c": 1 - c}
 
@@ -234,10 +241,22 @@
         cols = pl.ds(al(k * CW, CW), CW)
         lg[:, lg_cols(k)] = LT[pl.ds(al(x * T, 16), T), cols]
 
-    def task(k, r):
+    def part_of(rows, cols, dy):
+        deep = pl.ds(al(yn(dy) * NX * DB, DB), NX * DB)
+        return fdot(H[rows, deep], W5[deep, cols])
+
+    def early(k, r):
         rows = pl.ds(al(xp(r) * T, 16), T)
         cols = pl.ds(al(k * CW, CW), CW)
-        a = fdot(H[rows, :], W5[:, cols])
+        E[k, rows, :] = part_of(rows, cols, 0) + part_of(rows, cols, 1) + part_of(rows, cols, 3)
+
+    def task(k, r, rest=False):
+        rows = pl.ds(al(xp(r) * T, 16), T)
+        cols = pl.ds(al(k * CW, CW), CW)
+        if rest:
+            a = E[k, rows, :] + part_of(rows, cols, 2)
+        else:
+            a = fdot(H[rows, :], W5[:, cols])
         a = a + fdot(LI[rows, :], AU[:, cols])
         LT[rows, cols] = a.astype(BF16)
         top = jnp.max(a, axis=1, keepdims=True)
@@ -251,13 +270,14 @@
         old = jnp.where(lane128 == 12 + k, total, old)
         COL[rows, :] = jnp.where(lane128 == 16 + k, target, old)
 
-    def tasks(k0, nk, o0, no, out=True):
+    def turn(o):
+        return jnp.where(o == 2, 3, jnp.where(o == 3, 2, o))
+
+    def tasks(k0, nk, o0, no):
         def step(i, carry):
             k, o = k0 + i // no, o0 + lax.rem(i, no)
-            r = jnp.where(o == 2, 3, jnp.where(o == 3, 2, o))
+            r = turn(o)
             task(k, r)
-            if not out:
-                return carry
             if o0:
                 lg_remote(k, r)
             else:
@@ -266,6 +286,13 @@
             return carry
 
         lax.fori_loop(0, nk * no, step, 0)
+
+    def each_block(f):
+        def step(o, carry):
+            f(turn(o))
+            return carry
+
+        lax.fori_loop(0, NX, step, 0)
 
     loaded(WS, l_w)
     loaded(W5.at[own_rows, pl.ds(0, U)], l_own)
@@ -293,11 +320,10 @@
     phase("h_in13")
     h_in(1)
     h_in(3)
+    phase("p1b")
     y_fwd(1, 0)
-    phase("p1c")
     y_fwd(0, 1)
     y_fwd(0, 3)
-    phase("p1b")
     for r in ORDER:
         y_own(1, r)
     y_fwd(0, 2)
@@ -321,68 +347,74 @@
     lora_in(0)
     phase("h_fwd1")
     h_fwd(1)
-    phase("p1e")
+    phase("h_in2")
+    h_in(2)
+    phase("p1c")
     y_fwd(1, 1)
     y_fwd(1, 3)
-    phase("h_in2")
-    h_in(2)
-    phase("p1f")
+    phase("h_fwd3")
+    h_fwd(3)
+    phase("y_fwd1")
     y_fwd(1, 2)
+    phase("y_own2")
+    for r in ORDER:
+        y_own(2, r)
+    phase("h_last1")
+    h_last(1)
     phase("w_end0")
     w_end(0)
     phase("t0_0")
     tasks(0, 1, 0, 1)
-    phase("y_own2")
-    for r in ORDER:
-        y_own(2, r)
-    phase("h_fwd3")
-    h_fwd(3)
+    phase("h_end1")
+    h_end(1)
+    phase("t0_1")
+    lora_in(1)
+    tasks(0, 1, 1, 1)
     phase("y_own3")
     for r in ORDER:
         y_own(3, r)
     phase("w_end1")
     w_end(1)
-    phase("t1_0")
-    tasks(1, 1, 0, 1)
-    phase("h_last1")
-    h_last(1)
-    h_end(1)
-    phase("t01_1")
-    lora_in(1)
-    tasks(0, 2, 1, 1)
-    phase("y_fwd2")
-    for r in (0, 1, 3, 2):
-        y_fwd(2, r)
+    phase("t1_01")
+    tasks(1, 1, 0, 2)
     phase("h_fwd2")
     h_fwd(2)
+    phase("y_fwd2")
+    y_fwd(2, 0)
+    y_fwd(2, 1)
     phase("h_last3")
     h_last(3)
-    phase("y_fwd3")
-    y_fwd(3, 0)
-    y_fwd(3, 1)
-    phase("h_end3")
     h_end(3)
     phase("t01_3")
     lora_in(3)
     tasks(0, 2, 2, 1)
-    phase("y_fwd3b")
-    y_fwd(3, 3)
-    y_fwd(3, 2)
+    phase("y_fwd2b")
+    y_fwd(2, 3)
+    y_fwd(2, 2)
+    y_fwd(3, 0)
     phase("h_last2")
     h_last(2)
+    y_fwd(3, 1)
     h_end(2)
     phase("t01_2")
     lora_in(2)
     tasks(0, 2, 3, 1)
     sent(H.at[pl.ds(0, 3 * T), :], h_s)
+    phase("y_fwd3")
+    y_fwd(3, 3)
+    y_fwd(3, 2)
+    phase("w_near3")
+    w_near(3)
+    phase("t3a")
+    each_block(functools.partial(early, NK - 1))
     phase("w_end2")
     w_end(2)
     phase("t2")
     tasks(2, 1, 0, 4)
-    phase("w_end3")
-    w_end(3)
-    phase("t3")
-    tasks(3, 1, 0, 4, False)
+    phase("w_far3")
+    w_far(3)
+    phase("t3b")
+    each_block(functools.partial(task, NK - 1, rest=True))
     phase("stats_a")
 
     STA[v] = jnp.broadcast_to(jnp.ones((1, 1, 1), F32), (3, 16, 128))
@@ -447,7 +479,7 @@
                 G5[m, part, k * CW : (k + 1) * CW] = g.astype(BF16)
             return carry
 
-        lax.fori_loop(0, NX, step, 0)
+        lax.fori_loop(0, NX, step, 0, unroll=True)
         rows = G5[:, OFF[j] : OFF[j] + LEN[j], 0:U].reshape(NX * LEN[j], U)
         lora = tdot(rows, AU[...]).reshape(NX, LEN[j], 128)
         for m in range(NX):
@@ -458,7 +490,7 @@
             G5[m, part, U + 128 : U + 256] = (one - high.astype(F32)).astype(BF16)
 
     def send_rows(i):
-        part = pl.ds(OFF[2 * i], LEN[2 * i] * 2)
+        part = pl.ds(OFF[2 * i], LEN[2 * i] + LEN[2 * i + 1])
         for r in ORDER:
             send(G5.at[xn(r), part, pl.ds(0, U)], gr.at[part, pl.ds(my_cols, U)], gr_s, grs, {"x": xn(r)})
         gr[part, pl.ds(my_cols, U)] = G5[x, part, 0:U]
@@ -517,62 +549,41 @@
 
         lax.fori_loop(0, 2, step, 0)
 
-    phase("grad0")
-    gradient(0)
-    phase("core00")
-    for_core(0, 0)
-    phase("own00")
-    own(0, 0, mine)
-    phase("grad1")
-    gradient(1)
-    send_rows(0)
-    phase("core01")
-    for_core(0, 1)
-    phase("grad2")
-    gradient(2)
-    phase("own01")
-    own(0, 1, mine)
-    phase("core02")
-    for_core(0, 2)
-    phase("grad3")
-    gradient(3)
-    send_rows(1)
-    phase("own02")
-    own(0, 2, mine)
-    phase("core03")
-    for_core(0, 3)
-    for_core(1, 0)
-    phase("own03")
-    own(0, 3, mine)
-    phase("core1")
-    for j in range(1, NQ):
-        for_core(1, j)
-
-    phase("losses")
-    sums = [jnp.sum(jnp.where(jobs == float(j), loss, 0.0), axis=0, keepdims=True) for j in range(JOBS)]
-    JL[y] = jnp.concatenate(sums, axis=0)
-    for r in (1, 3, 2):
-        send(JL.at[y], JL.at[y], jn_s, jn, {"y": yn(r)})
-    for q in range(3):
-        n = min(128, T - q * 128)
-        t = COL2[pl.ds(al(x * T + q * 128, 8), n), :]
-        if n < 128:
-            t = jnp.concatenate([t, jnp.zeros((128 - n, 128), F32)], axis=0)
-        small[0:1, q * 128 : (q + 1) * 128] = t.T[3:4]
-    got(JL.at[0:3], jn)
-    total = jnp.sum(JL[0] + JL[1] + JL[2] + JL[3], axis=1, keepdims=True) / counts
-    total = jnp.concatenate([jnp.broadcast_to(total, (8, 128)), jnp.zeros((120, 128), F32)], axis=0)
-    small[0:1, 384:512] = total.T[0:1]
-
-    phase("ring")
-
-    def ring_step(s, carry):
-        for j in range(NQ):
-            own(s, j, with_ring)
-            for_core(s + 1, j)
-        return carry
-
-    lax.fori_loop(1, NZ - 1, ring_step, 0)
+    def losses_out():
+        phase("losses")
+        sums = [jnp.sum(jnp.where(jobs == float(j), loss, 0.0), axis=0, keepdims=True) for j in range(JOBS)]
+        JL[y] = jnp.concatenate(sums, axis=0)
+        for r in (1, 3, 2):
+            send(JL.at[y], JL.at[y], jn_s, jn, {"y": yn(r)})
+        for q in range(3):
+            n = min(128, T - q * 128)
+            t = COL2[pl.ds(al(x * T + q * 128, 8), n), :]
+            if n < 128:
+                t = jnp.concatenate([t, jnp.zeros((128 - n, 128), F32)], axis=0)
+            small[0:1, q * 128 : (q + 1) * 128] = t.T[3:4]
+
+    def losses_in():
+        phase("losses2")
+        got(JL.at[0:3], jn)
+        total = jnp.sum(JL[0] + JL[1] + JL[2] + JL[3], axis=1, keepdims=True) / counts
+        total = jnp.concatenate([jnp.broadcast_to(total, (8, 128)), jnp.zeros((120, 128), F32)], axis=0)
+        small[0:1, 384:512] = total.T[0:1]
+
+    first_units = (
+        "g0 c00 g1 r0 o00 c01 g2 o01 c02 g3 r1 o02 c03 c10 o03 c11 o10 c12 o11 c13 o12"
+        " c20 o13 c21 o20 c22 o21 c23 o22 c30 o23 c31"
+    )
+    for op in first_units.split():
+        phase(op)
+        n = [int(i) for i in op[1:]]
+        if op[0] == "g":
+            gradient(n[0])
+        elif op[0] == "r":
+            send_rows(n[0])
+        elif op[0] == "c":
+            for_core(*n)
+        else:
+            own(*n, with_ring if n[0] else mine)
 
     xr = take("r", NQ)
     ag = take("r", 3 * NQ)
@@ -600,30 +611,51 @@
         FO[part, :] = total.astype(BF16)
         for h in range(2):
             src = FO.at[part, pl.ds(h * CW, CW)]
-            for r in (2, 1, 3):
+            for r in (1, 3):
                 send(src, hg_at(z, j, h), ag_s, ag + j * 3 + r - 1, {"z": zn(r)})
             send(src, hg_at(z, j, h), cc_s, cc, other)
             hg_at(z, j, h)[...] = FO[part, h * CW : (h + 1) * CW]
 
-    def gather(j):
-        phase("gather%d" % j)
-        for r in (1, 3, 2):
-            got(hg.at[pl.ds(OFF[j], LEN[j]), pl.ds(0, SH)], ag + j * 3 + r - 1)
+    def pair_ref(j):
+        return hg.at[pl.ds(OFF[j], LEN[j]), pl.ds(0, SH)]
+
+    def relay(j):
+        phase("relay%d" % j)
+        for r in (1, 3):
+            got(pair_ref(j), ag + j * 3 + r - 1)
+            h = r // 2
+            src = hg_at(lax.rem(z + NZ - r, NZ), j, h)
+            send(src, src, ag_s, ag + j * 3 + 1, {"z": zn(r)})
             for h in range(2):
                 src = hg_at(lax.rem(z + NZ - r, NZ), j, h)
                 send(src, src, cc_s, cc, other)
 
+    def gather(j):
+        phase("gather%d" % j)
+        got(pair_ref(j), ag + j * 3 + 1)
+        for h in range(2):
+            src = hg_at(zn(2), j, h)
+            send(src, src, cc_s, cc, other)
+
     last(0)
+    for_core(3, 2)
     last(1)
     x_sum(0)
+    for_core(3, 3)
     last(2)
     x_sum(1)
+    relay(0)
     last(3)
+    losses_out()
     x_sum(2)
+    relay(1)
     gather(0)
     x_sum(3)
+    relay(2)
     gather(1)
+    relay(3)
     gather(2)
+    losses_in()
     gather(3)
 
     phase("arrivals")
@@ -648,7 +680,7 @@
     assert used == {"s": NSEND, "r": NRECV, "l": NLOAD}, used
 
 
-NSEND, NRECV, NLOAD = 14, 127, 5
+NSEND, NRECV, NLOAD = 14, 131, 5
 
 
 def emit(lgv, grv, hgv, small, lg, gr, hg, tl, jl, sem):

time: 174 us -> 167 us (0.960)
  Pallas kernels: 173 us -> 166 us
    pallas_call x1, Pallas kernels: 169 us -> 162 us  [shards(): pl.pallas_call(kernel, out_shape=(vmem(T, V), vmem(T, V), vmem(T, D), vme...]
where the time goes in v5:
time: 167 us
  Pallas kernels  166 us (99%)
    pallas_call x1, Pallas kernels, shards(): pl.pallas_call(kernel, out_shape=(vmem(T, V), vmem(T, V), vmem(T, D), vme...  162 us
    pallas_call x1, Pallas kernels, shards(): pl.pallas_call(emit, out_shape=(jax.ShapeDtypeStruct((T, V), BF16), jax.S...  4.07 us

profile of v5, /device:TPU:1, one launch (start us, length us, event | category | flops | bytes accessed | tf_op | source)
XLA Modules:
  0.0 167.3 jit_solution(6602073974228917084)
XLA Ops:
  0.6 162.4 %step.1 = (bf16[352,4096]{1,0:T(8,128)(2,1)S(1)}, bf16[352,4096]{1,0:T(8,128)(2,1)S(1)}, bf16[352,4096]{1,0:T(8,128)(2,1)S(1)}, f32[1,512]{1,0:T(1,128)S(1)}) custom-call(bf16[352,4096]{1,0:T(8,128)(2,1)} %hid.1, bf16[256,4096]{1,0:T(8,128)(2,1)} %w.1, bf16[4096,128]{1,0:T(8,128)(2,1)} %ad.1, bf16[128,4096]{1,0:T(8,128)(2,1)} %au.1, s32[352]{0:T(512)} %lab_in.1, ...), custom_call_target="tpu_custom_call" | custom-call | tf_op jit(solution)/shard_map/step/pallas_call | solution.py:706
  163.1 4.1 %emit.1 = (bf16[352,4096]{1,0:T(8,128)(2,1)}, bf16[352,4096]{1,0:T(8,128)(2,1)}, bf16[352,4096]{1,0:T(8,128)(2,1)}, f32[352]{0:T(512)}, f32[8]{0:T(128)}) custom-call(bf16[352,4096]{1,0:T(8,128)(2,1)S(1)} %get-tuple-element.9.lgv, bf16[352,4096]{1,0:T(8,128)(2,1)S(1)} %get-tuple-element.10.grv, bf16[352,4096]{1,0:T(8,128)(2,1)S(1)} %get-tuple-element.11.hgv, ...), custom_call_target="tpu_custom_call" | custom-call | tf_op jit(solution)/shard_map/emit/pallas_call | solution.py:741

commit v6 on v5

--- a/solution.py
+++ b/solution.py
@@ -19,9 +19,12 @@
 T = 352
 S = NX * T
 HT = T // 2
-LEN = (80, 112, 96, 64)
-OFF = (0, 80, 192, 288)
+LEN = (112, 96, 80, 64)
+OFF = (0, 112, 208, 288)
 NQ = len(LEN)
+NR = NQ - 1
+RT = OFF[NR]
+XT = LEN[NR]
 D = 4096
 DB = D // (NX * NY)
 V = 4096
@@ -44,7 +47,7 @@
 def kernel(
     hid, w, ad, au, lab_in, job_in,
     lg, gr, hg, small,
-    H, W5, WS, E, LT, G5, RR, XS, XR, FO, COL, COL2, LI, AU, AX, STA, STB, JR, CN, JL,
+    H, W5, WS, E, LT, G5, RR, XS, XR, XF, XFR, ZR, FO, COL, COL2, LI, AU, AX, STA, STB, TA, TB, JR, CN, JL,
     ssem, rsem, lsem,
 ):
     z, c, x, y = (lax.axis_index(a) for a in ("z", "c", "x", "y"))
@@ -135,12 +138,12 @@
     ORDER = (1, 3, 2)
     wx = take("r", NK * 3)
     hx = take("r", 3)
-    ax, lgs, cn, sa, sb, grs, jn, cc = (take("r") for _ in range(8))
+    ax, lgs, cn, sa, sb, ta, tb, grs, jn, cc, xf, zr = (take("r") for _ in range(12))
     wy = take("r", NK * 6)
     hz = take("r", 3 * 3)
     hc = take("r", 3)
-    ws_s, h_s, ax_s, lg_s, cn_s, sa_s, sb_s, gr_s, cs_s, ring_s, jn_s, x_s, ag_s, cc_s = (
-        take("s") for _ in range(14)
+    ws_s, h_s, ax_s, lg_s, cn_s, sa_s, sb_s, ta_s, tb_s, gr_s, cs_s, ring_s, jn_s, x_s, xf_s, zr_s, ag_s, cc_s = (
+        take("s") for _ in range(18)
     )
 
     def xp(r):
@@ -417,7 +420,8 @@
     each_block(functools.partial(task, NK - 1, rest=True))
     phase("stats_a")
 
-    STA[v] = jnp.broadcast_to(jnp.ones((1, 1, 1), F32), (3, 16, 128))
+    STA[v] = jnp.broadcast_to(jnp.ones((1, 1, 1), F32), (2, 16, 128))
+    TA[v] = jnp.zeros((16, 128), F32)
     JR[...] = jnp.full((16, 128), -1.0, F32)
     for b in range(NB):
         t = COL[b * 128 : (b + 1) * 128, :].T
@@ -425,12 +429,14 @@
         top = jnp.max(m, axis=0, keepdims=True)
         STA[v, 0, b : b + 1, :] = top
         STA[v, 1, b : b + 1, :] = jnp.sum(e * jnp.exp(m - top), axis=0, keepdims=True)
-        STA[v, 2, b : b + 1, :] = jnp.sum(g, axis=0, keepdims=True)
+        TA[v, b : b + 1, :] = jnp.sum(g, axis=0, keepdims=True)
         JR[b : b + 1, :] = t[1:2]
     turns = [(a, b) for a in (2, 1, 3, 0) for b in range(NC) if a or b]
     for a, b in turns:
         dev = {"z": zn(a), "c": lax.rem(c + b, NC)}
         send(STA.at[v], STA.at[v], sa_s, sa, dev)
+    for a, b in turns:
+        send(TA.at[v], TA.at[v], ta_s, ta, {"z": zn(a), "c": lax.rem(c + b, NC)})
     phase("counts")
     got(CN.at[0:3], cn)
     counts = jnp.sum(CN[0] + CN[1] + CN[2] + CN[3], axis=1, keepdims=True)
@@ -445,10 +451,9 @@
 
     def joined(ref, n):
         top = functools.reduce(jnp.maximum, [ref[i, 0] for i in range(n)])
-        e = functools.reduce(jnp.add, [ref[i, 1] * jnp.exp(ref[i, 0] - top) for i in range(n)])
-        return top, e, functools.reduce(jnp.add, [ref[i, 2] for i in range(n)])
-
-    STB[x, 0], STB[x, 1], STB[x, 2] = joined(STA, NZ * NC)
+        return top, functools.reduce(jnp.add, [ref[i, 1] * jnp.exp(ref[i, 0] - top) for i in range(n)])
+
+    STB[x, 0], STB[x, 1] = joined(STA, NZ * NC)
     phase("stats_b")
     for r in (2, 1, 3):
         send(STB.at[x], STB.at[x], sb_s, sb, {"x": xn(r)})
@@ -457,29 +462,38 @@
     lg_local(NK - 1)
     got(STB.at[0:3], sb)
     phase("finish")
-    top, e, g = joined(STB, NX)
-    loss = top + jnp.log(e) - g
+    top, e = joined(STB, NX)
     scaled = weight / e
-    blank = jnp.zeros((124, 128), F32)
+    blank = jnp.zeros((125, 128), F32)
     for b in range(NB):
-        parts = [i[b : b + 1] for i in (top, scaled, weight, loss)]
+        parts = [i[b : b + 1] for i in (top, scaled, weight)]
         COL2[b * 128 : (b + 1) * 128, :] = jnp.concatenate(parts + [blank], axis=0).T
+
+    def targets():
+        got(TA.at[0:7], ta)
+        TB[x] = functools.reduce(jnp.add, [TA[i] for i in range(NZ * NC)])
+        for r in (2, 1, 3):
+            send(TB.at[x], TB.at[x], tb_s, tb, {"x": xn(r)})
+
+    row_cw = lax.broadcasted_iota(jnp.int32, (1, CW), 1)
 
     def gradient(j):
         part = pl.ds(OFF[j], LEN[j])
 
         def step(m, carry):
             rows = pl.ds(al(m * T + OFF[j], 16), LEN[j])
-            lab = COL[rows, 0:1]
+            cols = COL[rows, :]
+            lab = cols[:, 0:1]
             weight = COL2[rows, 2:3]
+            factors = jnp.exp(cols - COL2[rows, 0:1]) * COL2[rows, 1:2]
             for k in range(NK):
-                f = jnp.exp(COL[rows, 8 + k : 9 + k] - COL2[rows, 0:1]) * COL2[rows, 1:2]
-                ids = (lane_cw[: LEN[j]] + (base + k * CW)).astype(F32)
-                g = E[k, rows, :] * f - jnp.where(ids == lab, weight, 0.0)
+                ids = (row_cw + (base + k * CW)).astype(F32)
+                g = E[k, rows, :] * factors[:, 8 + k : 9 + k] - jnp.where(lab == ids, weight, 0.0)
                 G5[m, part, k * CW : (k + 1) * CW] = g.astype(BF16)
             return carry
 
         lax.fori_loop(0, NX, step, 0, unroll=True)
+        phase("lora%d" % j)
         rows = G5[:, OFF[j] : OFF[j] + LEN[j], 0:U].reshape(NX * LEN[j], U)
         lora = tdot(rows, AU[...]).reshape(NX, LEN[j], 128)
         for m in range(NX):
@@ -496,7 +510,7 @@
         gr[part, pl.ds(my_cols, U)] = G5[x, part, 0:U]
 
     cs_r = take("r", 32)
-    ring_r = take("r", 24)
+    ring_r = take("r", 6 * NR)
 
     def zt(s, h):
         return lax.rem(z + NZ + (2 * h - 1) * (s + 1), NZ)
@@ -517,7 +531,7 @@
         return rcopy(ps(s, h, j), ps(s, h, j, D // 2), cs_s, cs_r + i, other)
 
     def ring_copy(s, h, j):
-        i = (s * 2 + h) * NQ + j
+        i = (s * 2 + h) * NR + j
         return rcopy(
             RR.at[s, h, span(j)], RR.at[s + 1, h, span(j)], ring_s, ring_r + i,
             {"z": lax.rem(z + NZ + 1 - 2 * h, NZ)},
@@ -549,18 +563,45 @@
 
         lax.fori_loop(0, 2, step, 0)
 
+    def own_x(s):
+        def step(h, carry):
+            cols = pl.ds(al(zt(s, h) * SH + h * CW, CW), CW)
+            XF[:, :, cols] = mine(s, h, NR).astype(BF16).reshape(NX, XT, CW)
+            return carry
+
+        lax.fori_loop(0, 2, step, 0)
+
+    def x_first():
+        for r in (2, 1, 3):
+            send(XF.at[xn(r)], XFR.at[r - 1], xf_s, xf, {"x": xn(r)})
+
+    def x_first_sum():
+        phase("xf_sum")
+        got(XFR, xf)
+        total = XF[x].astype(F32)
+        for r in (1, 3, 2):
+            total = total + XFR[r - 1].astype(F32)
+        XF[x] = total.astype(BF16)
+        for r in (2, 1, 3):
+            send(XF.at[x, :, pl.ds(al(zn(r) * SH, SH), SH)], ZR.at[r - 1], zr_s, zr, {"z": zn(r)})
+
     def losses_out():
         phase("losses")
+        got(TB.at[0:3], tb)
+        loss = top + jnp.log(e) - (TB[0] + TB[1] + TB[2] + TB[3])
         sums = [jnp.sum(jnp.where(jobs == float(j), loss, 0.0), axis=0, keepdims=True) for j in range(JOBS)]
         JL[y] = jnp.concatenate(sums, axis=0)
         for r in (1, 3, 2):
             send(JL.at[y], JL.at[y], jn_s, jn, {"y": yn(r)})
+        for b in range(NB):
+            row = jnp.concatenate([loss[b : b + 1], jnp.zeros((127, 128), F32)], axis=0)
+            COL2[b * 128 : (b + 1) * 128, :] = row.T
         for q in range(3):
             n = min(128, T - q * 128)
             t = COL2[pl.ds(al(x * T + q * 128, 8), n), :]
             if n < 128:
                 t = jnp.concatenate([t, jnp.zeros((128 - n, 128), F32)], axis=0)
-            small[0:1, q * 128 : (q + 1) * 128] = t.T[3:4]
+            small[0:1, q * 128 : (q + 1) * 128] = t.T[0:1]
 
     def losses_in():
         phase("losses2")
@@ -569,11 +610,9 @@
         total = jnp.concatenate([jnp.broadcast_to(total, (8, 128)), jnp.zeros((120, 128), F32)], axis=0)
         small[0:1, 384:512] = total.T[0:1]
 
-    first_units = (
-        "g0 c00 g1 r0 o00 c01 g2 o01 c02 g3 r1 o02 c03 c10 o03 c11 o10 c12 o11 c13 o12"
-        " c20 o13 c21 o20 c22 o21 c23 o22 c30 o23 c31"
-    )
-    for op in first_units.split():
+    units = ("g0 c00 g1 r0", "o00 c01 g2 o01", "c02 g3 o02 c03", "c10 c13 o10 c11", "c23 o11 c12 c33")
+    units = units + ("f0 o12 f1 f2", "f3 x t c20", "c21 o20 c22 o21", "c30 o22 c31")
+    for op in " ".join(units).split():
         phase(op)
         n = [int(i) for i in op[1:]]
         if op[0] == "g":
@@ -582,10 +621,16 @@
             send_rows(n[0])
         elif op[0] == "c":
             for_core(*n)
+        elif op[0] == "f":
+            own_x(n[0])
+        elif op[0] == "x":
+            x_first()
+        elif op[0] == "t":
+            targets()
         else:
             own(*n, with_ring if n[0] else mine)
 
-    xr = take("r", NQ)
+    xr = take("r", NR)
     ag = take("r", 3 * NQ)
 
     def hg_at(zz, j, h):
@@ -609,6 +654,19 @@
         for r in (1, 3, 2):
             total = total + XR[r - 1, part, :].astype(F32)
         FO[part, :] = total.astype(BF16)
+        push(j)
+
+    def z_sum():
+        phase("zsum")
+        got(ZR, zr)
+        total = XF[x, :, pl.ds(al(z * SH, SH), SH)].astype(F32)
+        for r in (1, 3, 2):
+            total = total + ZR[r - 1].astype(F32)
+        FO[RT:T, :] = total.astype(BF16)
+        push(NR)
+
+    def push(j):
+        part = pl.ds(OFF[j], LEN[j])
         for h in range(2):
             src = FO.at[part, pl.ds(h * CW, CW)]
             for r in (1, 3):
@@ -639,24 +697,24 @@
 
     last(0)
     for_core(3, 2)
+    x_first_sum()
     last(1)
     x_sum(0)
-    for_core(3, 3)
     last(2)
+    send_rows(1)
+    z_sum()
     x_sum(1)
     relay(0)
-    last(3)
+    x_sum(2)
+    relay(3)
     losses_out()
-    x_sum(2)
     relay(1)
     gather(0)
-    x_sum(3)
+    gather(3)
+    losses_in()
     relay(2)
     gather(1)
-    relay(3)
     gather(2)
-    losses_in()
-    gather(3)
 
     phase("arrivals")
     got(lg.at[:, pl.ds(0, 3 * U)], lgs)
@@ -674,20 +732,25 @@
     sent(RR.at[0:3], ring_s)
     sent(JL.at[0:3], jn_s)
     sent(XR, x_s)
-    sent(XR, ag_s)
+    sent(XFR, xf_s)
+    sent(ZR, zr_s)
+    sent(hg.at[:, pl.ds(0, 3 * SH)], ag_s)
+    sent(TA.at[0:7], ta_s)
+    sent(TB.at[0:3], tb_s)
     sent(hg.at[:, pl.ds(0, NZ * SH)], cc_s)
     phase(None)
     assert used == {"s": NSEND, "r": NRECV, "l": NLOAD}, used
 
 
-NSEND, NRECV, NLOAD = 14, 131, 5
+NSEND, NRECV, NLOAD = 18, 128, 5
 
 
 def emit(lgv, grv, hgv, small, lg, gr, hg, tl, jl, sem):
-    copies = [
-        pltpu.make_async_copy(src, dst, sem.at[i])
-        for i, (src, dst) in enumerate(((lgv, lg), (grv, gr), (hgv, hg)))
-    ]
+    copies = []
+    for src, dst in ((lgv, lg), (grv, gr), (hgv, hg)):
+        for i in range(4):
+            part = pl.ds(i * 88, 88)
+            copies.append(pltpu.make_async_copy(src.at[part], dst.at[part], sem.at[len(copies)]))
     for d in copies:
         d.start()
     tl[...] = small[0, :T]
@@ -715,17 +778,22 @@
             vmem(NK, S, CW, dtype=F32),
             vmem(S, U),
             vmem(NX, T, U + 256),
-            vmem(NZ, 2, S, CW),
-            vmem(NX, T, SH),
-            vmem(3, T, SH),
+            vmem(NZ, 2, NX * RT, CW),
+            vmem(NX, RT, SH),
+            vmem(3, RT, SH),
+            vmem(NX, XT, NZ * SH),
+            vmem(3, XT, NZ * SH),
+            vmem(3, XT, SH),
             vmem(T, SH),
             vmem(S, 128, dtype=F32),
             vmem(S, 128, dtype=F32),
             vmem(S, 128),
             vmem(128, U),
             vmem(NX, 3, 8, 128, dtype=F32),
-            vmem(NZ * NC, 3, 16, 128, dtype=F32),
-            vmem(NX, 3, 16, 128, dtype=F32),
+            vmem(NZ * NC, 2, 16, 128, dtype=F32),
+            vmem(NX, 2, 16, 128, dtype=F32),
+            vmem(NZ * NC, 16, 128, dtype=F32),
+            vmem(NX, 16, 128, dtype=F32),
             vmem(16, 128, dtype=F32),
             vmem(NY, 8, 128, dtype=F32),
             vmem(NY, 8, 128, dtype=F32),
@@ -734,7 +802,7 @@
             pltpu.SemaphoreType.DMA((NLOAD,)),
         ],
         compiler_params=pltpu.CompilerParams(
-            collective_id=0, has_side_effects=True, vmem_limit_bytes=52 * 1024 * 1024
+            collective_id=0, has_side_effects=True, vmem_limit_bytes=53 * 1024 * 1024
         ),
         name="step",
     )(hidden, weight, down, up, labels, jobs)
@@ -749,7 +817,7 @@
         ),
         in_specs=[vm] * 4,
         out_specs=(hbm, hbm, hbm, vm, vm),
-        scratch_shapes=[pltpu.SemaphoreType.DMA((3,))],
+        scratch_shapes=[pltpu.SemaphoreType.DMA((12,))],
         compiler_params=pltpu.CompilerParams(vmem_limit_bytes=1024 * 1024),
         name="emit",
     )(*(pltpu.with_memory_space_constraint(i, pltpu.VMEM) for i in held))

time: 167 us -> 160 us (0.958)
  Pallas kernels: 166 us -> 159 us
    pallas_call x1, Pallas kernels: 162 us -> 155 us  [shards(): pl.pallas_call(kernel, out_shape=(vmem(T, V), vmem(T, V), vmem(T, D), vme...]
where the time goes in v6:
time: 160 us; the launch traced here: 159 us
  Pallas kernels  159 us (99%)
    pallas_call x1, Pallas kernels, shards(): pl.pallas_call(kernel, out_shape=(vmem(T, V), vmem(T, V), vmem(T, D), vme...  155 us
    pallas_call x1, Pallas kernels, shards(): pl.pallas_call(emit, out_shape=(jax.ShapeDtypeStruct((T, V), BF16), jax.S...  4.04 us

profile of v6, /device:TPU:1, one launch (start us, length us, event | category | flops | bytes accessed | tf_op | source)
XLA Modules:
  0.0 159.5 jit_solution(138170604880062107)
XLA Ops:
  0.6 154.6 %step.1 = (bf16[352,4096]{1,0:T(8,128)(2,1)S(1)}, bf16[352,4096]{1,0:T(8,128)(2,1)S(1)}, bf16[352,4096]{1,0:T(8,128)(2,1)S(1)}, f32[1,512]{1,0:T(1,128)S(1)}) custom-call(bf16[352,4096]{1,0:T(8,128)(2,1)} %hid.1, bf16[256,4096]{1,0:T(8,128)(2,1)} %w.1, bf16[4096,128]{1,0:T(8,128)(2,1)} %ad.1, bf16[128,4096]{1,0:T(8,128)(2,1)} %au.1, s32[352]{0:T(512)} %lab_in.1, ...), custom_call_target="tpu_custom_call" | custom-call | tf_op jit(solution)/shard_map/step/pallas_call | solution.py:769
  155.2 4.0 %emit.1 = (bf16[352,4096]{1,0:T(8,128)(2,1)}, bf16[352,4096]{1,0:T(8,128)(2,1)}, bf16[352,4096]{1,0:T(8,128)(2,1)}, f32[352]{0:T(512)}, f32[8]{0:T(128)}) custom-call(bf16[352,4096]{1,0:T(8,128)(2,1)S(1)} %get-tuple-element.9.lgv, bf16[352,4096]{1,0:T(8,128)(2,1)S(1)} %get-tuple-element.10.grv, bf16[352,4096]{1,0:T(8,128)(2,1)S(1)} %get-tuple-element.11.hgv, ...), custom_call_target="tpu_custom_call" | custom-call | tf_op jit(solution)/shard_map/emit/pallas_call | solution.py:809

commit v7 on v6

--- a/solution.py
+++ b/solution.py
@@ -19,8 +19,8 @@
 T = 352
 S = NX * T
 HT = T // 2
-LEN = (112, 96, 80, 64)
-OFF = (0, 112, 208, 288)
+LEN = (112, 112, 48, 80)
+OFF = (0, 112, 224, 272)
 NQ = len(LEN)
 NR = NQ - 1
 RT = OFF[NR]
@@ -47,7 +47,7 @@
 def kernel(
     hid, w, ad, au, lab_in, job_in,
     lg, gr, hg, small,
-    H, W5, WS, E, LT, G5, RR, XS, XR, XF, XFR, ZR, FO, COL, COL2, LI, AU, AX, STA, STB, TA, TB, JR, CN, JL,
+    H, W5, WS, E, LT, G5, RR, XS, XR, XQ, XF, XFR, XP, ZR, FO, COL, COL2, LI, AU, AX, STA, STB, TA, TB, JR, CN, JL,
     ssem, rsem, lsem,
 ):
     z, c, x, y = (lax.axis_index(a) for a in ("z", "c", "x", "y"))
@@ -138,7 +138,8 @@
     ORDER = (1, 3, 2)
     wx = take("r", NK * 3)
     hx = take("r", 3)
-    ax, lgs, cn, sa, sb, ta, tb, grs, jn, cc, xf, zr = (take("r") for _ in range(12))
+    ax, lgs, cn, sa, sb, ta, tb, grs, jn, cc, zr = (take("r") for _ in range(11))
+    xf = take("r", 3)
     wy = take("r", NK * 6)
     hz = take("r", 3 * 3)
     hc = take("r", 3)
@@ -571,16 +572,30 @@
 
         lax.fori_loop(0, 2, step, 0)
 
+    XH = NZ * SH // 2
+
+    def xcols(i):
+        return pl.ds(i * XH, XH)
+
     def x_first():
-        for r in (2, 1, 3):
-            send(XF.at[xn(r)], XFR.at[r - 1], xf_s, xf, {"x": xn(r)})
+        far = XF.at[xn(2)]
+        send(far.at[:, xcols(0)], XP.at[0], xf_s, xf, {"x": xn(1)})
+        send(far.at[:, xcols(1)], XP.at[1], xf_s, xf + 1, {"x": xn(3)})
+        send(XF.at[xn(1), :, xcols(1)], XFR.at[0, :, xcols(1)], xf_s, xf + 2, {"x": xn(1)})
+        send(XF.at[xn(3), :, xcols(0)], XFR.at[1, :, xcols(0)], xf_s, xf + 2, {"x": xn(3)})
+
+    def x_first_mid():
+        for i, r in ((0, 1), (1, 3)):
+            got(XP.at[i], xf + i)
+            cols = slice(i * XH, (i + 1) * XH)
+            both = XF[xn(r), :, cols].astype(F32) + XP[i].astype(F32)
+            XF[xn(r), :, cols] = both.astype(BF16)
+            send(XF.at[xn(r), :, xcols(i)], XFR.at[i, :, xcols(i)], xf_s, xf + 2, {"x": xn(r)})
 
     def x_first_sum():
         phase("xf_sum")
-        got(XFR, xf)
-        total = XF[x].astype(F32)
-        for r in (1, 3, 2):
-            total = total + XFR[r - 1].astype(F32)
+        got(XFR, xf + 2)
+        total = XF[x].astype(F32) + XFR[0].astype(F32) + XFR[1].astype(F32)
         XF[x] = total.astype(BF16)
         for r in (2, 1, 3):
             send(XF.at[x, :, pl.ds(al(zn(r) * SH, SH), SH)], ZR.at[r - 1], zr_s, zr, {"z": zn(r)})
@@ -611,7 +626,7 @@
         small[0:1, 384:512] = total.T[0:1]
 
     units = ("g0 c00 g1 r0", "o00 c01 g2 o01", "c02 g3 o02 c03", "c10 c13 o10 c11", "c23 o11 c12 c33")
-    units = units + ("f0 o12 f1 f2", "f3 x t c20", "c21 o20 c22 o21", "c30 o22 c31")
+    units = units + ("f0 o12 f1 f2", "f3 x t c20", "c21 o20 c22 o21", "m c30 o22 c31")
     for op in " ".join(units).split():
         phase(op)
         n = [int(i) for i in op[1:]]
@@ -625,12 +640,14 @@
             own_x(n[0])
         elif op[0] == "x":
             x_first()
+        elif op[0] == "m":
+            x_first_mid()
         elif op[0] == "t":
             targets()
         else:
             own(*n, with_ring if n[0] else mine)
 
-    xr = take("r", NR)
+    xr = take("r", 3 * NR)
     ag = take("r", 3 * NQ)
 
     def hg_at(zz, j, h):
@@ -643,16 +660,29 @@
         for h in range(2):
             a = with_ring(NZ - 1, h, j)
             XS[:, OFF[j] : OFF[j] + LEN[j], h * CW : (h + 1) * CW] = a.astype(BF16).reshape(NX, LEN[j], CW)
-        for r in (2, 1, 3):
-            send(XS.at[xn(r), part], XR.at[r - 1, part], x_s, xr + j, {"x": xn(r)})
+        far = XS.at[xn(2), part]
+        at = xr + j * 3
+        send(far.at[:, pl.ds(0, CW)], XQ.at[0, part], x_s, at, {"x": xn(1)})
+        send(far.at[:, pl.ds(CW, CW)], XQ.at[1, part], x_s, at + 1, {"x": xn(3)})
+        send(XS.at[xn(1), part, pl.ds(CW, CW)], XR.at[0, part, pl.ds(CW, CW)], x_s, at + 2, {"x": xn(1)})
+        send(XS.at[xn(3), part, pl.ds(0, CW)], XR.at[1, part, pl.ds(0, CW)], x_s, at + 2, {"x": xn(3)})
+
+    def x_mid(j):
+        part = pl.ds(OFF[j], LEN[j])
+        phase("xmid%d" % j)
+        at = xr + j * 3
+        for i, r in ((0, 1), (1, 3)):
+            got(XQ.at[i, part], at + i)
+            cols = pl.ds(i * CW, CW)
+            both = XS[xn(r), part, cols].astype(F32) + XQ[i, part, :].astype(F32)
+            XS[xn(r), part, cols] = both.astype(BF16)
+            send(XS.at[xn(r), part, cols], XR.at[i, part, cols], x_s, at + 2, {"x": xn(r)})
 
     def x_sum(j):
         part = pl.ds(OFF[j], LEN[j])
         phase("xsum%d" % j)
-        got(XR.at[:, part], xr + j)
-        total = XS[x, part, :].astype(F32)
-        for r in (1, 3, 2):
-            total = total + XR[r - 1, part, :].astype(F32)
+        got(XR.at[:, part], xr + j * 3 + 2)
+        total = XS[x, part, :].astype(F32) + XR[0, part, :].astype(F32) + XR[1, part, :].astype(F32)
         FO[part, :] = total.astype(BF16)
         push(j)
 
@@ -697,28 +727,33 @@
 
     last(0)
     for_core(3, 2)
+    x_mid(0)
     x_first_sum()
     last(1)
     x_sum(0)
     last(2)
+    x_mid(1)
+    x_mid(2)
     send_rows(1)
     z_sum()
     x_sum(1)
     relay(0)
     x_sum(2)
     relay(3)
-    losses_out()
     relay(1)
     gather(0)
+    relay(2)
     gather(3)
-    losses_in()
-    relay(2)
+    losses_out()
     gather(1)
     gather(2)
+    losses_in()
 
     phase("arrivals")
     got(lg.at[:, pl.ds(0, 3 * U)], lgs)
+    phase("arr_gr")
     got(gr.at[:, pl.ds(0, 3 * U)], grs)
+    phase("arr_hg")
     got(hg.at[:, pl.ds(0, NZ * SH)], cc)
     phase("drain")
     sent(W5.at[pl.ds(0, 60 * DB // NX), pl.ds(0, U)], ws_s)
@@ -731,8 +766,8 @@
     sent(H.at[:, pl.ds(0, D // 2)], cs_s)
     sent(RR.at[0:3], ring_s)
     sent(JL.at[0:3], jn_s)
-    sent(XR, x_s)
-    sent(XFR, xf_s)
+    sent(XS.at[0:3], x_s)
+    sent(XF.at[0:3], xf_s)
     sent(ZR, zr_s)
     sent(hg.at[:, pl.ds(0, 3 * SH)], ag_s)
     sent(TA.at[0:7], ta_s)
@@ -742,7 +777,7 @@
     assert used == {"s": NSEND, "r": NRECV, "l": NLOAD}, used
 
 
-NSEND, NRECV, NLOAD = 18, 128, 5
+NSEND, NRECV, NLOAD = 18, 136, 5
 
 
 def emit(lgv, grv, hgv, small, lg, gr, hg, tl, jl, sem):
@@ -780,9 +815,11 @@
             vmem(NX, T, U + 256),
             vmem(NZ, 2, NX * RT, CW),
             vmem(NX, RT, SH),
-            vmem(3, RT, SH),
+            vmem(2, RT, SH),
+            vmem(2, RT, CW),
             vmem(NX, XT, NZ * SH),
-            vmem(3, XT, NZ * SH),
+            vmem(2, XT, NZ * SH),
+            vmem(2, XT, NZ * SH // 2),
             vmem(3, XT, SH),
             vmem(T, SH),
             vmem(S, 128, dtype=F32),

time: 160 us -> 159 us (level)
  no operation moved by 1% of the time
where the time goes in v7:
time: 159 us; the launch traced here: 158 us
  Pallas kernels  158 us (99%)
    pallas_call x1, Pallas kernels, shards(): pl.pallas_call(kernel, out_shape=(vmem(T, V), vmem(T, V), vmem(T, D), vme...  154 us
    pallas_call x1, Pallas kernels, shards(): pl.pallas_call(emit, out_shape=(jax.ShapeDtypeStruct((T, V), BF16), jax.S...  4.04 us

profile of v7, /device:TPU:1, one launch (start us, length us, event | category | flops | bytes accessed | tf_op | source)
XLA Modules:
  0.0 158.4 jit_solution(10692152517424586071)
XLA Ops:
  0.6 153.6 %step.1 = (bf16[352,4096]{1,0:T(8,128)(2,1)S(1)}, bf16[352,4096]{1,0:T(8,128)(2,1)S(1)}, bf16[352,4096]{1,0:T(8,128)(2,1)S(1)}, f32[1,512]{1,0:T(1,128)S(1)}) custom-call(bf16[352,4096]{1,0:T(8,128)(2,1)} %hid.1, bf16[256,4096]{1,0:T(8,128)(2,1)} %w.1, bf16[4096,128]{1,0:T(8,128)(2,1)} %ad.1, bf16[128,4096]{1,0:T(8,128)(2,1)} %au.1, s32[352]{0:T(512)} %lab_in.1, ...), custom_call_target="tpu_custom_call" | custom-call | tf_op jit(solution)/shard_map/step/pallas_call | solution.py:804
  154.2 4.0 %emit.1 = (bf16[352,4096]{1,0:T(8,128)(2,1)}, bf16[352,4096]{1,0:T(8,128)(2,1)}, bf16[352,4096]{1,0:T(8,128)(2,1)}, f32[352]{0:T(512)}, f32[8]{0:T(128)}) custom-call(bf16[352,4096]{1,0:T(8,128)(2,1)S(1)} %get-tuple-element.9.lgv, bf16[352,4096]{1,0:T(8,128)(2,1)S(1)} %get-tuple-element.10.grv, bf16[352,4096]{1,0:T(8,128)(2,1)S(1)} %get-tuple-element.11.hgv, ...), custom_call_target="tpu_custom_call" | custom-call | tf_op jit(solution)/shard_map/emit/pallas_call | solution.py:846

commit v8 on v7

--- a/solution.py
+++ b/solution.py
@@ -727,11 +727,11 @@
 
     last(0)
     for_core(3, 2)
+    last(1)
     x_mid(0)
     x_first_sum()
-    last(1)
+    last(2)
     x_sum(0)
-    last(2)
     x_mid(1)
     x_mid(2)
     send_rows(1)

time: 159 us -> 159 us (level)
  no operation moved by 1% of the time
where the time goes in v8:
time: 159 us
  Pallas kernels  158 us (99%)
    pallas_call x1, Pallas kernels, shards(): pl.pallas_call(kernel, out_shape=(vmem(T, V), vmem(T, V), vmem(T, D), vme...  154 us
    pallas_call x1, Pallas kernels, shards(): pl.pallas_call(emit, out_shape=(jax.ShapeDtypeStruct((T, V), BF16), jax.S...  4.04 us

profile of v8, /device:TPU:1, one launch (start us, length us, event | category | flops | bytes accessed | tf_op | source)
XLA Modules:
  0.0 159.2 jit_solution(2937648494801720610)
XLA Ops:
  0.6 154.3 %step.1 = (bf16[352,4096]{1,0:T(8,128)(2,1)S(1)}, bf16[352,4096]{1,0:T(8,128)(2,1)S(1)}, bf16[352,4096]{1,0:T(8,128)(2,1)S(1)}, f32[1,512]{1,0:T(1,128)S(1)}) custom-call(bf16[352,4096]{1,0:T(8,128)(2,1)} %hid.1, bf16[256,4096]{1,0:T(8,128)(2,1)} %w.1, bf16[4096,128]{1,0:T(8,128)(2,1)} %ad.1, bf16[128,4096]{1,0:T(8,128)(2,1)} %au.1, s32[352]{0:T(512)} %lab_in.1, ...), custom_call_target="tpu_custom_call" | custom-call | tf_op jit(solution)/shard_map/step/pallas_call | solution.py:804
  155.0 4.0 %emit.1 = (bf16[352,4096]{1,0:T(8,128)(2,1)}, bf16[352,4096]{1,0:T(8,128)(2,1)}, bf16[352,4096]{1,0:T(8,128)(2,1)}, f32[352]{0:T(512)}, f32[8]{0:T(128)}) custom-call(bf16[352,4096]{1,0:T(8,128)(2,1)S(1)} %get-tuple-element.9.lgv, bf16[352,4096]{1,0:T(8,128)(2,1)S(1)} %get-tuple-element.10.grv, bf16[352,4096]{1,0:T(8,128)(2,1)S(1)} %get-tuple-element.11.hgv, ...), custom_call_target="tpu_custom_call" | custom-call | tf_op jit(solution)/shard_map/emit/pallas_call | solution.py:846

commit v9 on v7

--- a/solution.py
+++ b/solution.py
@@ -277,11 +277,11 @@
     def turn(o):
         return jnp.where(o == 2, 3, jnp.where(o == 3, 2, o))
 
-    def tasks(k0, nk, o0, no):
+    def tasks(k0, nk, o0, no, rest=False):
         def step(i, carry):
             k, o = k0 + i // no, o0 + lax.rem(i, no)
             r = turn(o)
-            task(k, r)
+            task(k, r, rest)
             if o0:
                 lg_remote(k, r)
             else:
@@ -407,14 +407,18 @@
     phase("y_fwd3")
     y_fwd(3, 3)
     y_fwd(3, 2)
+    phase("w_near2")
+    w_near(2)
+    phase("t2a")
+    each_block(functools.partial(early, NK - 2))
     phase("w_near3")
     w_near(3)
     phase("t3a")
     each_block(functools.partial(early, NK - 1))
-    phase("w_end2")
-    w_end(2)
-    phase("t2")
-    tasks(2, 1, 0, 4)
+    phase("w_far2")
+    w_far(2)
+    phase("t2b")
+    tasks(2, 1, 0, 4, True)
     phase("w_far3")
     w_far(3)
     phase("t3b")

time: 159 us -> 157 us (0.987)
  no operation moved by 1% of the time
where the time goes in v9:
time: 157 us
  Pallas kernels  157 us (100%)
    pallas_call x1, Pallas kernels, shards(): pl.pallas_call(kernel, out_shape=(vmem(T, V), vmem(T, V), vmem(T, D), vme...  152 us
    pallas_call x1, Pallas kernels, shards(): pl.pallas_call(emit, out_shape=(jax.ShapeDtypeStruct((T, V), BF16), jax.S...  4.04 us

profile of v9, /device:TPU:1, one launch (start us, length us, event | category | flops | bytes accessed | tf_op | source)
XLA Modules:
  0.0 157.3 jit_solution(15132116881029919800)
XLA Ops:
  0.6 152.5 %step.1 = (bf16[352,4096]{1,0:T(8,128)(2,1)S(1)}, bf16[352,4096]{1,0:T(8,128)(2,1)S(1)}, bf16[352,4096]{1,0:T(8,128)(2,1)S(1)}, f32[1,512]{1,0:T(1,128)S(1)}) custom-call(bf16[352,4096]{1,0:T(8,128)(2,1)} %hid.1, bf16[256,4096]{1,0:T(8,128)(2,1)} %w.1, bf16[4096,128]{1,0:T(8,128)(2,1)} %ad.1, bf16[128,4096]{1,0:T(8,128)(2,1)} %au.1, s32[352]{0:T(512)} %lab_in.1, ...), custom_call_target="tpu_custom_call" | custom-call | tf_op jit(solution)/shard_map/step/pallas_call | solution.py:808
  153.1 4.0 %emit.1 = (bf16[352,4096]{1,0:T(8,128)(2,1)}, bf16[352,4096]{1,0:T(8,128)(2,1)}, bf16[352,4096]{1,0:T(8,128)(2,1)}, f32[352]{0:T(512)}, f32[8]{0:T(128)}) custom-call(bf16[352,4096]{1,0:T(8,128)(2,1)S(1)} %get-tuple-element.9.lgv, bf16[352,4096]{1,0:T(8,128)(2,1)S(1)} %get-tuple-element.10.grv, bf16[352,4096]{1,0:T(8,128)(2,1)S(1)} %get-tuple-element.11.hgv, ...), custom_call_target="tpu_custom_call" | custom-call | tf_op jit(solution)/shard_map/emit/pallas_call | solution.py:850
